TPU v7x, 256 devices: a whole 4x4x8 slice. The times are simulated.
256 devices in a mesh: obs: 64 (over z, y_hi, x), chan: 4 (over y_lo, core).
Axes of the slice: x: 4, y: 4 (y_hi: 2, y_lo: 2; y = y_hi * 2 + y_lo), z: 8, core: 2. Of those that a mesh axis runs over, the one named last changes fastest.
Arguments:
- departures: bfloat16 [8192, 131072], P('chan', 'obs'), may hold values from -8 to 8
- predictors: bfloat16 [10, 131072], P(None, 'obs'), may hold values from -3 to 3
- inv_band: bfloat16 [63, 8192], P(None, 'chan'), may hold values from -1 to 2.5
- band_id: int32 [8192], replicated, may hold values from 0 to 340, never falling along the last dimension, each value on 1 to 32 neighbouring positions
- line_counts: int32 [1024], P('obs'), may hold values from 24 to 128
Outputs:
- gram: float32 [100, 8192], P(None, ('chan', 'obs'))
- rhs: float32 [10, 8192], P(None, ('chan', 'obs'))
Inputs may be any that keep to these rules, and one draw needn't show every extreme that they name: `band_id`: band numbers never fall along the channels; a band spans 1 to 32 channels. `line_counts`: slots of a scan line at or beyond its count are empty.
All inputs are finite; a program needn't handle non-finite values.
Results may differ from a plain program's by a relative error of at most 0.00062.
Values may be sent and summed in bfloat16 or wider, within the bound.
A program may use at most 64 MiB of HBM per device.

v0:
```python
import jax
import jax.numpy as jnp
from jax import lax
from jax.sharding import PartitionSpec as P

huber_edge = 1.0


def with_halo(cells, sides, width):
    for axis, dim in sides:
        count = lax.axis_size(axis)
        ends = count - 1
        head = lax.slice_in_dim(cells, 0, width, axis=dim)
        tail = lax.slice_in_dim(cells, cells.shape[dim] - width, cells.shape[dim], axis=dim)
        cells = jnp.concatenate(
            [
                lax.ppermute(tail, axis, [(i, (i + 1) % count) for i in range(ends)]),
                cells,
                lax.ppermute(head, axis, [((i + 1) % count, i) for i in range(ends)]),
            ],
            axis=dim,
        )
    return cells


def in_blocks(value, dim, count):
    shape = value.shape
    parts = value.reshape(*shape[:dim], count, shape[dim] // count, *shape[dim + 1 :])
    return jnp.moveaxis(parts, dim, 0)


def sum_at_owner(value, axis, dim):
    parts = in_blocks(value, dim, lax.axis_size(axis))
    arrived = lax.all_to_all(parts, axis, split_axis=0, concat_axis=0, tiled=True)
    return arrived.astype(jnp.float32).sum(axis=0)


def in_one_piece(arrays, axis, dim, along):
    both = jnp.concatenate(arrays, axis=along)
    filled, at, finished = (sum_at_owner(both, axis, dim), 0, [])
    for a in arrays:
        finished.append(lax.slice_in_dim(filled, at, at + a.shape[along], axis=along))
        at += a.shape[along]
    return tuple(finished)


def on_device(departures, predictors, inv_band, band_id, line_counts):
    own, obs_dev = departures.shape
    count_pred = predictors.shape[0]
    half = inv_band.shape[0] // 2
    tile = min(256, own)
    tiles = own // tile
    extent = tile + 2 * half
    padded = with_halo(departures, (("chan", 0),), half)
    base = lax.axis_index("chan") * own
    marked = jnp.pad(band_id, (half, half), constant_values=-1)
    near_all = lax.dynamic_slice_in_dim(marked, base, own + 2 * half)
    line_slots = obs_dev // line_counts.shape[0]
    live = (
        (jnp.arange(line_slots, dtype=jnp.int32)[None, :] < line_counts[:, None])
        .reshape(obs_dev)
        .astype(jnp.float32)
    )
    band_rows = inv_band.T.reshape(tiles, tile, 2 * half + 1)
    widened = jnp.pad(band_rows, ((0, 0), (0, 0), (0, extent + 1 - (2 * half + 1))))
    skewed = widened.reshape(tiles, tile * (extent + 1))[:, : tile * extent].reshape(
        tiles, tile, extent
    )
    pieces = []
    for number in range(tiles):
        own_ids = near_all[half + number * tile : half + (number + 1) * tile]
        near_ids = near_all[number * tile : number * tile + extent]
        same = own_ids[:, None] == near_ids[None, :]
        matrix = jnp.where(same, skewed[number], jnp.zeros_like(skewed[number]))
        window = padded[number * tile : number * tile + extent]
        pieces.append(jnp.dot(matrix, window, preferred_element_type=jnp.float32))
    weighted = jnp.concatenate(pieces, axis=0)
    ratio = live[None, :] * (huber_edge / jnp.maximum(jnp.abs(weighted), huber_edge))
    qc_weight = ratio.astype(jnp.bfloat16)
    scaled = (ratio * weighted).astype(jnp.bfloat16)
    pred_wide = predictors.astype(jnp.float32)
    pairs = (
        (pred_wide[:, None, :] * pred_wide[None, :, :])
        .reshape(count_pred * count_pred, obs_dev)
        .astype(jnp.bfloat16)
    )
    factor = 1.0 / float(obs_dev * lax.axis_size("obs"))
    gram_terms = (
        jnp.einsum("ko,co->kc", pairs, qc_weight, preferred_element_type=jnp.float32) * factor
    )
    rhs_terms = (
        jnp.einsum("ko,co->kc", predictors, scaled, preferred_element_type=jnp.float32) * factor
    )
    gram_part, rhs_part = in_one_piece(
        (gram_terms.astype(jnp.bfloat16), rhs_terms.astype(jnp.bfloat16)), "obs", 1, 0
    )
    return (gram_part, rhs_part)


def solution(mesh):
    in_specs = (P("chan", "obs"), P(None, "obs"), P(None, "chan"), P(), P("obs"))
    out_specs = (P(None, ("chan", "obs")), P(None, ("chan", "obs")))
    return jax.shard_map(
        on_device, mesh=mesh, in_specs=in_specs, out_specs=out_specs, check_vma=False
    )
```

profile of v0, /device:TPU:1, one launch (start us, length us, event | category | flops | bytes accessed | tf_op | source)
XLA Modules:
  0.0 78.5 jit_solution(13482402502233052283)
XLA Ops:
  0.6 0.0 copy-start.3
  0.6 0.0 copy-start.1
  0.7 0.0 copy-start
  0.7 1.0 %fusion.57 = (bf16[31,2048]{1,0:T(8,128)(2,1)S(1)}, bf16[31,2048]{1,0:T(8,128)(2,1)S(1)}) fusion(bf16[2048,2048]{1,0:T(8,128)(2,1)} %param.5), kind=kLoop, calls=%fused_computation.101 | loop fusion | bytes 507904 | tf_op jit(solution)/shard_map/slice | solution.py:13
  1.7 4.6 %collective-permute-start = (bf16[31,2048]{1,0:T(8,128)(2,1)S(1)}, bf16[31,2048]{1,0:T(8,128)(2,1)S(1)}, u32[]{:S(2)}, u32[]{:S(2)}) collective-permute-start(bf16[31,2048]{1,0:T(8,128)(2,1)S(1)} %get-tuple-element.17), channel_id=1, source_target_pairs={{0,1},{1,2},{2,3},{4,5},{5,6},{6,7},{8,9},{9,10},{10,11},{12,13},{... | collective-permute-start | bytes 380936 | tf_op jit(solution)/shard_map/ppermute | solution.py:17
  6.3 1.9 %collective-permute-start.1 = (bf16[31,2048]{1,0:T(8,128)(2,1)S(1)}, bf16[31,2048]{1,0:T(8,128)(2,1)S(1)}, u32[]{:S(2)}, u32[]{:S(2)}) collective-permute-start(bf16[31,2048]{1,0:T(8,128)(2,1)S(1)} %get-tuple-element.16), channel_id=1, source_target_pairs={{1,0},{2,1},{3,2},{5,4},{6,5},{7,6},{9,8},{10,9},{11,10},{13,12},{... | collective-permute-start | bytes 380936 | tf_op jit(solution)/shard_map/ppermute | solution.py:19
  8.2 1.3 %copy.14 = bf16[2048,63]{1,0:T(8,128)(2,1)S(1)} copy(bf16[2048,63]{0,1:T(8,128)(2,1)} %bitcast.16) | data formatting | bytes 516096 | tf_op jit(solution)/shard_map/reshape | solution.py:64
  9.5 0.2 pad.9
  9.7 2.4 %reshape.82 = bf16[653312]{0:T(1024)(128)(2,1)S(1)} reshape(bf16[8,256,319]{2,1,0:T(8,128)(2,1)S(1)} %pad.9) | data formatting | bytes 2613248
  12.2 1.4 %reshape.71 = bf16[8,81664]{1,0:T(8,128)(2,1)S(1)} reshape(bf16[653312]{0:T(1024)(128)(2,1)S(1)} %reshape.82) | data formatting | bytes 2613248 | tf_op jit(solution)/shard_map/reshape | solution.py:66
  13.6 9.3 %slice_reduce_fusion = (bf16[81408]{0:T(1024)(128)(2,1)S(1)}, bf16[81408]{0:T(1024)(128)(2,1)S(1)}, bf16[81408]{0:T(1024)(128)(2,1)S(1)}, bf16[81408]{0:T(1024)(...) fusion(bf16[8,81664]{1,0:T(8,128)(2,1)S(1)} %reshape.71), kind=kLoop, calls=%fused_computation.39 | loop fusion | bytes 2605056 | tf_op jit(solution)/shard_map/slice | solution.py:74
  22.9 0.0 copy-done.3
  22.9 0.1 convert_bitcast_fusion
  22.9 0.0 copy-done.1
  23.0 0.1 multiply_convert_fusion.8
  23.1 0.0 copy-done
  23.1 0.1 pad_dynamic-slice_fusion
  23.2 0.5 squeeze.24
  23.7 0.5 squeeze.25
  24.2 0.5 squeeze.26
  24.6 0.5 squeeze.27
  25.1 0.5 squeeze.28
  25.6 0.5 squeeze.29
  26.1 0.5 squeeze.30
  26.5 0.5 squeeze.31
  27.0 0.1 convert_element_type.41
  27.2 0.1 pad_dynamic-slice_fusion.15
  27.3 0.0 collective-permute-done
  27.3 2.2 %convolution_dynamic-update-slice_fusion.7 = f32[2048,2048]{1,0:T(8,128)S(1)} fusion(bf16[2048,2048]{1,0:T(8,128)(2,1)} %param.5, bf16[31,2048]{1,0:T(8,128)(2,1)S(1)} %collective-permute-done, bf16[256,318]{1,0:T(8,128)(2,1)S(1)} %squeeze.24, s32[318]{0:T(512)S(1)} %get-tuple-element.27, s32[256]{0:T(256)S(1)} %get-tuple-element.19), kind=kOutput, calls=%fused_computation.12 | convolution fusion | flops 336215040 | bytes 10777848 | tf_op jit(solution)/shard_map/dot_general | solution.py:76
  29.5 0.0 slice-start.1
  29.5 2.2 %convolution_dynamic-update-slice_fusion.6 = f32[2048,2048]{1,0:T(8,128)S(1)} fusion(f32[2048,2048]{1,0:T(8,128)S(1)} %convolution_dynamic-update-slice_fusion.7, bf16[2048,2048]{1,0:T(8,128)(2,1)} %param.5, bf16[256,318]{1,0:T(8,128)(2,1)S(1)} %squeeze.25, s32[318]{0:T(512)S(1)} %get-tuple-element.28, s32[256]{0:T(256)S(1)} %get-tuple-element.20), kind=kOutput, calls=%fused_computation.11 | convolution fusion | flops 333609984 | bytes 3607552 | tf_op jit(solution)/shard_map/dot_general | solution.py:76
  31.8 2.1 %convolution_dynamic-update-slice_fusion.5 = f32[2048,2048]{1,0:T(8,128)S(1)} fusion(f32[2048,2048]{1,0:T(8,128)S(1)} %convolution_dynamic-update-slice_fusion.6, bf16[2048,2048]{1,0:T(8,128)(2,1)} %param.5, bf16[256,318]{1,0:T(8,128)(2,1)S(1)} %squeeze.26, s32[318]{0:T(512)S(1)} %get-tuple-element.29, s32[256]{0:T(256)S(1)} %get-tuple-element.21), kind=kOutput, calls=%fused_computation.10 | convolution fusion | flops 333609984 | bytes 3607552 | tf_op jit(solution)/shard_map/dot_general | solution.py:76
  33.9 2.1 %convolution_dynamic-update-slice_fusion.4 = f32[2048,2048]{1,0:T(8,128)S(1)} fusion(f32[2048,2048]{1,0:T(8,128)S(1)} %convolution_dynamic-update-slice_fusion.5, bf16[2048,2048]{1,0:T(8,128)(2,1)} %param.5, bf16[256,318]{1,0:T(8,128)(2,1)S(1)} %squeeze.27, s32[318]{0:T(512)S(1)} %get-tuple-element.30, s32[256]{0:T(256)S(1)} %get-tuple-element.22), kind=kOutput, calls=%fused_computation.9 | convolution fusion | flops 333609984 | bytes 3607552 | tf_op jit(solution)/shard_map/dot_general | solution.py:76
  36.0 0.0 slice-done
  36.0 0.0 slice-done.1
  36.0 0.8 convolution_dynamic-update-slice_fusion.3
  36.8 0.8 convolution_dynamic-update-slice_fusion.2
  37.5 0.8 convolution_dynamic-update-slice_fusion.1
  38.3 0.0 collective-permute-done.1
  38.3 0.8 convolution_dynamic-update-slice_fusion
  39.1 3.2 %fusion.12 = bf16[10,2048]{1,0:T(8,128)(2,1)S(1)} fusion(bf16[10,2048]{1,0:T(8,128)(2,1)S(1)} %copy-done.1, f32[2048,2048]{1,0:T(8,128)S(1)} %convolution_dynamic-update-slice_fusion, f32[2048]{0:T(1024)S(1)} %convert_bitcast_fusion), kind=kOutput, calls=%fused_computation.17 | convolution fusion | flops 109092864 | bytes 16867328 | tf_op jit(solution)/shard_map/ko,co->kc/dot_general | solution.py:92
  42.3 3.3 %fusion.7 = bf16[100,2048]{1,0:T(8,128)(2,1)S(1)} fusion(bf16[100,2048]{1,0:T(8,128)(2,1)S(1)} %convert_element_type.41, f32[2048,2048]{1,0:T(8,128)S(1)} %convolution_dynamic-update-slice_fusion, f32[2048]{0:T(1024)S(1)} %convert_bitcast_fusion), kind=kOutput, calls=%fused_computation.14 | convolution fusion | flops 860241920 | bytes 17604608 | tf_op jit(solution)/shard_map/ko,co->kc/dot_general | solution.py:89
  45.6 0.3 copy.12
  45.9 31.7 %all_to_all.5 = bf16[64,110,32]{1,2,0:T(8,128)(2,1)S(1)} all-to-all(bf16[64,110,32]{1,2,0:T(8,128)(2,1)S(1)} %bitcast.15), channel_id=1, replica_groups=mesh['obs'=64,'chan'=4] {'obs'}, dimensions={0} | all-to-all | bytes 901120 | tf_op jit(solution)/shard_map/all_to_all | solution.py:34
  77.6 0.1 convert_reduce_fusion
  77.7 0.1 slice.172
  77.8 0.7 copy.13
  78.5 0.0 copy-done.2
  (5 shorter events, 0.1 us)
Async XLA Ops:
  0.6 22.2 %copy-start.3 = (s32[16]{0:T(128)S(1)}, s32[16]{0:T(128)}, u32[]{:S(2)}) copy-start(s32[16]{0:T(128)} %param.9) | copy-start | bytes 196
  0.6 22.3 %copy-start.1 = (bf16[10,2048]{1,0:T(8,128)(2,1)S(1)}, bf16[10,2048]{1,0:T(8,128)(2,1)}, u32[]{:S(2)}) copy-start(bf16[10,2048]{1,0:T(8,128)(2,1)} %param.6) | copy-start | bytes 122884
  0.7 22.4 %copy-start = (s32[8192]{0:T(1024)S(1)}, s32[8192]{0:T(1024)}, u32[]{:S(2)}) copy-start(s32[8192]{0:T(1024)} %param.8) | copy-start | bytes 98308
  1.7 25.6 %collective-permute-start = (bf16[31,2048]{1,0:T(8,128)(2,1)S(1)}, bf16[31,2048]{1,0:T(8,128)(2,1)S(1)}, u32[]{:S(2)}, u32[]{:S(2)}) collective-permute-start(bf16[31,2048]{1,0:T(8,128)(2,1)S(1)} %get-tuple-element.17), channel_id=1, source_target_pairs={{0,1},{1,2},{2,3},{4,5},{5,6},{6,7},{8,9},{9,10},{10,11},{12,13},{... | collective-permute-start | bytes 380936 | tf_op jit(solution)/shard_map/ppermute | solution.py:17
  6.3 32.0 %collective-permute-start.1 = (bf16[31,2048]{1,0:T(8,128)(2,1)S(1)}, bf16[31,2048]{1,0:T(8,128)(2,1)S(1)}, u32[]{:S(2)}, u32[]{:S(2)}) collective-permute-start(bf16[31,2048]{1,0:T(8,128)(2,1)S(1)} %get-tuple-element.16), channel_id=1, source_target_pairs={{1,0},{2,1},{3,2},{5,4},{6,5},{7,6},{9,8},{10,9},{11,10},{13,12},{... | collective-permute-start | bytes 380936 | tf_op jit(solution)/shard_map/ppermute | solution.py:19
  27.3 8.7 %slice-start = ((s8[8388608]{0:T(1024)(128)(4,1)}), s8[4194304]{0:T(1024)(128)(4,1)S(1)}, s32[]{:S(2)}) async-start(s8[8388608]{0:T(1024)(128)(4,1)} %bitcast.12), calls=%async_computation.1 | async-start | bytes 8388608
  29.5 6.5 %slice-start.1 = ((s8[8388608]{0:T(1024)(128)(4,1)}), s8[4194304]{0:T(1024)(128)(4,1)S(1)}, s32[]{:S(2)}) async-start(s8[8388608]{0:T(1024)(128)(4,1)} %bitcast.12), calls=%async_computation.2 | async-start | bytes 8388608
  77.7 0.8 copy-start.2
where the time goes:
time: 78.8 us; the launch traced here: 78.5 us
  blocking collectives  31.7 us (40%)
  local copies, waits for them, and re-layouts  20.9 us (27%)
  matrix products  18.2 us (23%)
  starting transfers between devices  6.5 us (8%)
  between operations  0.92 us (1%)
    all_to_all x1, blocking collectives, sum_at_owner(): lax.all_to_all(parts, axis, split_axis=0, concat_axis=0, tiled=True)  31.7 us
    dot_general x8, matrix products, on_device(): pieces.append(jnp.dot(matrix, window, preferred_element_type=jnp.float32))  11.7 us
    slice x1, local copies, waits for them, and re-layouts, on_device(): matrix = jnp.where(same, skewed[number], jnp.zeros_like(skewed[number]))  9.3 us
    ppermute x1, starting transfers between devices, with_halo(): lax.ppermute(tail, axis, [(i, (i + 1) % count) for i in range(ends)])  4.58 us
    squeeze x8, local copies, waits for them, and re-layouts, on_device(): matrix = jnp.where(same, skewed[number], jnp.zeros_like(skewed[number]))  3.75 us
    dot_general x1, matrix products, on_device(): jnp.einsum('ko,co->kc', pairs, qc_weight, preferred_element_type=jnp.floa...  3.25 us
    dot_general x1, matrix products, on_device(): jnp.einsum('ko,co->kc', predictors, scaled, preferred_element_type=jnp.fl...  3.25 us
    unnamed x14, local copies, waits for them, and re-layouts  3.15 us
  transfers between devices with their start and end apart: 2, of which 0 were waited for; matrix products, arithmetic and copies ran while one was open for 38% of the time, Pallas kernels for 0%

commit v1 on v0

v1 whole, which is shorter than its diff:
```python
import functools

import jax
import jax.numpy as jnp
import numpy as np
from jax import lax
from jax.experimental import pallas as pl
from jax.experimental.pallas import tpu as pltpu
from jax.sharding import PartitionSpec as P

MESH = pl.DeviceIdType.MESH
PRED = 10
HALO = 32
BLOCK = 256
WINDOW = 192
PAIRS = [(j, k) for j in range(PRED) for k in range(j, PRED)]
MAIN = 64


def selectors():
    left = np.zeros((16, 128), np.float32)
    right = np.zeros((16, 128), np.float32)
    alone = np.zeros((16, 256), np.float32)
    for half in range(2):
        for m, (j, k) in enumerate(PAIRS):
            left[j, half * MAIN + m] = 1
            right[k, half * MAIN + m] = 1
        for k in range(PRED - 1):
            alone[k, half * MAIN + len(PAIRS) + k] = 1
    alone[PRED - 1, 128:] = 1
    return np.concatenate([left, right, alone], axis=1)


def kernel(
    dep_ref, pred_ref, inv_ref, ids_ref, lines_ref, sel_ref,
    gram_ref, rhs_ref,
    cells, wq, ws, inv_t, id_rows, id_cols, send1, recv1, own, send2, recv2,
    load_sem, halo_send, halo_recv, send1_sem, recv1_sem, send2_sem, recv2_sem,
):
    obs = lax.axis_index("obs")
    chan = lax.axis_index("chan")
    z, p = obs // 8, obs % 8
    rows = dep_ref.shape[0]
    blocks = rows // BLOCK
    factor = 1.0 / float(dep_ref.shape[1] * lax.axis_size("obs"))
    last = lax.axis_size("chan") - 1
    turn = 1 - 2 * (z // 4)

    def block_at(step):
        return (z + turn * (step + 1) + 2 * blocks) % blocks

    def load(number):
        at = pl.multiple_of(number * BLOCK, BLOCK)
        return pltpu.make_async_copy(
            dep_ref.at[pl.ds(at, BLOCK)],
            cells.at[pl.ds(pl.multiple_of(at + HALO, HALO), BLOCK)],
            load_sem.at[number],
        )

    def piece(order):
        return (z + turn * order + 2 * blocks) % blocks

    for order in range(blocks):
        load(piece(order)).start()

    barrier = pltpu.get_barrier_semaphore()
    for d in range(1, 8):
        pl.semaphore_signal(barrier, inc=1, device_id=((z + d) % 8 * 8 + p, chan), device_id_type=MESH)
        pl.semaphore_signal(barrier, inc=1, device_id=(z * 8 + (p + d) % 8, chan), device_id_type=MESH)

    @pl.when(chan > 0)
    def _():
        pl.semaphore_signal(barrier, inc=1, device_id=(obs, chan - 1), device_id_type=MESH)

    @pl.when(chan < last)
    def _():
        pl.semaphore_signal(barrier, inc=1, device_id=(obs, chan + 1), device_id_type=MESH)

    here = pl.multiple_of(chan * 16, 16)
    id_rows[pl.ds(8, 16), :] = ids_ref[pl.ds(here, 16), :].astype(jnp.float32)
    before = ids_ref[pl.ds(jnp.maximum(here - 1, 0), 1), :].astype(jnp.float32)
    after = ids_ref[pl.ds(jnp.minimum(here + 16, 16 * last + 15), 1), :].astype(jnp.float32)
    id_rows[pl.ds(7, 1), :] = jnp.where(chan > 0, before, -1.0)
    id_rows[pl.ds(24, 1), :] = jnp.where(chan < last, after, -1.0)
    lane16 = lax.broadcasted_iota(jnp.int32, (16, 128), 1)
    turned = [pltpu.roll(id_rows[pl.ds(7 + n, 16), :], 32, axis=1) for n in range(3)]
    id_cols[:, 0:128] = jnp.where(lane16 < 32, turned[0], turned[1])
    id_cols[:, 128:256] = jnp.where(lane16 < 32, turned[1], turned[2])

    @pl.loop(0, 16)
    def _(s):
        at = pl.multiple_of(s * 128, 128)
        entries = inv_ref[:, pl.ds(at, 128)].astype(jnp.float32)
        number = jnp.broadcast_to(id_rows[pl.ds(8 + s, 1), :], (64, 128))
        stacked = jnp.concatenate([entries, jnp.zeros((1, 128), jnp.float32), number], axis=0)
        inv_t[pl.ds(at, 128), :] = stacked.T

    @pl.loop(0, 16)
    def _(s):
        at = pl.multiple_of(s * 128, 128)
        lane = lax.broadcasted_iota(jnp.int32, (PRED, 128), 1)
        values = pred_ref[:, pl.ds(at, 128)].astype(jnp.float32)
        values = jnp.where(lane < lines_ref[s], values, 0.0)
        values = jnp.concatenate([values, jnp.zeros((16 - PRED, 128), jnp.float32)], axis=0)
        picked = jnp.dot(
            values.T.astype(jnp.bfloat16), sel_ref[...], preferred_element_type=jnp.float32
        )
        products = (picked[:, 0:128] * picked[:, 128:256]).astype(jnp.bfloat16)
        wq[pl.ds(at, 128), :] = jnp.concatenate([products, jnp.zeros_like(products)], axis=1)
        ws[pl.ds(at, 128), :] = picked[:, 256:512].astype(jnp.bfloat16)

    pl.semaphore_wait(barrier, 14 + jnp.minimum(chan, 1) + jnp.minimum(last - chan, 1))

    def up():
        return pltpu.make_async_remote_copy(
            src_ref=dep_ref.at[pl.ds(0, HALO)],
            dst_ref=cells.at[pl.ds(HALO + rows, HALO)],
            send_sem=halo_send.at[0],
            recv_sem=halo_recv.at[0],
            device_id=(obs, jnp.maximum(chan - 1, 0)),
            device_id_type=MESH,
        )

    def down():
        return pltpu.make_async_remote_copy(
            src_ref=dep_ref.at[pl.ds(rows - HALO, HALO)],
            dst_ref=cells.at[pl.ds(0, HALO)],
            send_sem=halo_send.at[1],
            recv_sem=halo_recv.at[1],
            device_id=(obs, jnp.minimum(chan + 1, last)),
            device_id_type=MESH,
        )

    @pl.when(chan > 0)
    def _():
        up().start()

    @pl.when(chan < last)
    def _():
        down().start()

    @pl.when(chan == 0)
    def _():
        cells[pl.ds(0, HALO), :] = jnp.zeros((HALO, cells.shape[1]), jnp.bfloat16)

    @pl.when(chan == last)
    def _():
        cells[pl.ds(HALO + rows, HALO), :] = jnp.zeros((HALO, cells.shape[1]), jnp.bfloat16)

    def to_plane(number):
        return pltpu.make_async_remote_copy(
            src_ref=send1.at[number],
            dst_ref=recv1.at[z],
            send_sem=send1_sem,
            recv_sem=recv1_sem,
            device_id=(number * 8 + p, chan),
            device_id_type=MESH,
        )

    def band(first):
        lane = lax.broadcasted_iota(jnp.int32, (128, 128), 1)
        both = inv_t[pl.ds(first, 128), :]
        entries = jnp.where(lane < 64, both, 0.0)
        number = jnp.where(lane < 64, pltpu.roll(both, 64, axis=1), both)
        wide = jnp.concatenate([entries, jnp.zeros_like(entries)], axis=1)
        wide = pltpu.roll(wide, 1, axis=1, stride=1, stride_axis=0)
        near = id_cols[pl.ds(first // 128, 1), :]
        same = jnp.concatenate([number, number], axis=1) == near
        return jnp.where(same, wide, 0.0).astype(jnp.bfloat16)[:, 0:WINDOW]

    load(piece(0)).wait()
    load(piece(1)).wait()

    @pl.loop(0, blocks)
    def _(step):
        number = block_at(step)

        @pl.when(step < blocks - 2)
        def _():
            load(piece(step + 2)).wait()

        @pl.when((number == 0) & (chan > 0))
        def _():
            down().wait_recv()

        @pl.when((number == blocks - 1) & (chan < last))
        def _():
            up().wait_recv()

        first = pl.multiple_of(number * BLOCK, BLOCK)
        matrices = [band(first + 128 * n) for n in range(2)]
        total = jnp.zeros((BLOCK, 256), jnp.float32)
        for part in range(cells.shape[1] // 256):
            cols = pl.ds(part * 256, 256)
            weighted = jnp.concatenate(
                [
                    jnp.dot(
                        matrices[n],
                        cells[pl.ds(pl.multiple_of(first + 128 * n, 128), WINDOW), cols],
                        preferred_element_type=jnp.float32,
                    )
                    for n in range(2)
                ],
                axis=0,
            )
            weight = (1.0 / jnp.maximum(jnp.abs(weighted), 1.0)).astype(jnp.bfloat16)
            scaled = jnp.clip(weighted, -1.0, 1.0).astype(jnp.bfloat16)
            total = total + jnp.dot(weight, wq[cols, :], preferred_element_type=jnp.float32)
            total = total + jnp.dot(scaled, ws[cols, :], preferred_element_type=jnp.float32)

        lane = lax.broadcasted_iota(jnp.int32, (8, 16, 128), 2)
        halves = total[:, 0:128].reshape(8, 2, 16, 128)
        main = jnp.where(lane < MAIN, halves[:, 0], halves[:, 1]).reshape(16, 8, 128)
        tenth = total[:, 128:256].reshape(8, 32, 128)
        on = lax.broadcasted_iota(jnp.int32, (8, 32, 128), 2) == lax.broadcasted_iota(
            jnp.int32, (8, 32, 128), 1
        )
        tenth = jnp.sum(jnp.where(on, tenth, 0.0), axis=1)
        own[0:16] = main
        own[16] = tenth
        send1[number, 0:16] = main.astype(jnp.bfloat16)
        send1[number, 16] = tenth.astype(jnp.bfloat16)

        @pl.when(step < blocks - 1)
        def _():
            to_plane(number).start()

    def wait_for(buffer, sem):
        pltpu.make_async_copy(buffer.at[pl.ds(0, 7)], buffer.at[pl.ds(0, 7)], sem).wait()

    wait_for(recv1, recv1_sem)
    sums = own[...]
    for source in range(8):
        came = recv1[source].astype(jnp.float32)
        sums = sums + jnp.where(source == z, jnp.zeros_like(came), came)
    for peer in range(8):
        send2[peer, 0:2] = sums[2 * peer : 2 * peer + 2]
        send2[peer, 2] = sums[16]

    @pl.loop(1, 8)
    def _(d):
        peer = (p + d) % 8
        pltpu.make_async_remote_copy(
            src_ref=send2.at[peer],
            dst_ref=recv2.at[p],
            send_sem=send2_sem,
            recv_sem=recv2_sem,
            device_id=(z * 8 + peer, chan),
            device_id_type=MESH,
        ).start()

    mine = send2[p]
    wait_for(recv2, recv2_sem)
    whole = mine
    for source in range(8):
        came = recv2[source]
        whole = whole + jnp.where(source == p, jnp.zeros_like(came), came)
    whole = whole * factor
    flat = whole[0:2].reshape(16, 128).T
    values = jnp.concatenate([flat[0:MAIN], flat[MAIN:128]], axis=1)
    index = {pair: m for m, pair in enumerate(PAIRS)}
    for j in range(PRED):
        for k in range(PRED):
            m = index[(min(j, k), max(j, k))]
            gram_ref[pl.ds(j * PRED + k, 1), :] = values[m : m + 1, :]
    rhs_ref[0 : PRED - 1, :] = values[len(PAIRS) : MAIN, :]
    row = lax.broadcasted_iota(jnp.int32, (8, 128), 0)
    tenth = jnp.sum(jnp.where(row == p, whole[2], 0.0), axis=0, keepdims=True)
    rhs_ref[PRED - 1 : PRED, :] = tenth[:, 0:32]

    wait_for(send1, send1_sem)
    wait_for(send2, send2_sem)

    @pl.when(chan > 0)
    def _():
        up().wait_send()

    @pl.when(chan < last)
    def _():
        down().wait_send()


def on_device(departures, predictors, inv_band, band_id, line_counts):
    rows, obs_dev = departures.shape
    owned = rows // lax.axis_size("obs")
    vmem = pl.BlockSpec(memory_space=pltpu.VMEM)
    return pl.pallas_call(
        kernel,
        out_shape=(
            jax.ShapeDtypeStruct((PRED * PRED, owned), jnp.float32),
            jax.ShapeDtypeStruct((PRED, owned), jnp.float32),
        ),
        in_specs=[
            pl.BlockSpec(memory_space=pltpu.HBM),
            vmem,
            vmem,
            vmem,
            pl.BlockSpec(memory_space=pltpu.SMEM),
            vmem,
        ],
        out_specs=(vmem, vmem),
        scratch_shapes=[
            pltpu.VMEM((rows + 2 * HALO, obs_dev), jnp.bfloat16),
            pltpu.VMEM((obs_dev, 256), jnp.bfloat16),
            pltpu.VMEM((obs_dev, 256), jnp.bfloat16),
            pltpu.VMEM((rows, 128), jnp.float32),
            pltpu.VMEM((32, 128), jnp.float32),
            pltpu.VMEM((16, 256), jnp.float32),
            pltpu.VMEM((8, 17, 8, 128), jnp.bfloat16),
            pltpu.VMEM((8, 17, 8, 128), jnp.bfloat16),
            pltpu.VMEM((17, 8, 128), jnp.float32),
            pltpu.VMEM((8, 3, 8, 128), jnp.float32),
            pltpu.VMEM((8, 3, 8, 128), jnp.float32),
            pltpu.SemaphoreType.DMA((8,)),
            pltpu.SemaphoreType.DMA((2,)),
            pltpu.SemaphoreType.DMA((2,)),
            pltpu.SemaphoreType.DMA,
            pltpu.SemaphoreType.DMA,
            pltpu.SemaphoreType.DMA,
            pltpu.SemaphoreType.DMA,
        ],
        compiler_params=pltpu.CompilerParams(collective_id=0, has_side_effects=True),
        name="normal_equations",
    )(
        departures,
        predictors,
        inv_band,
        band_id.reshape(band_id.shape[0] // 128, 128),
        line_counts,
        jnp.asarray(selectors(), jnp.bfloat16),
    )


def solution(mesh):
    in_specs = (P("chan", "obs"), P(None, "obs"), P(None, "chan"), P(), P("obs"))
    out_specs = (P(None, ("chan", "obs")), P(None, ("chan", "obs")))
    return jax.shard_map(
        on_device, mesh=mesh, in_specs=in_specs, out_specs=out_specs, check_vma=False
    )
```

time: 78.8 us -> 39.4 us (0.50)
  Pallas kernels: 0 us -> 35.7 us
  blocking collectives: 31.7 us -> 0 us
  matrix products: 18.2 us -> 0 us
  local copies, waits for them, and re-layouts: 20.9 us -> 2.79 us
  starting transfers between devices: 6.5 us -> 0 us
    pallas_call x0 -> x1, Pallas kernels: none -> 35.7 us  [on_device(): pl.pallas_call(kernel, out_shape=(jax.ShapeDtypeStruct((PRED * PRED, owne...]
    all_to_all x1 -> x0, blocking collectives: 31.7 us -> none  [sum_at_owner(): lax.all_to_all(parts, axis, split_axis=0, concat_axis=0, tiled=True)]
    dot_general x10 -> x0, matrix products: 18.2 us -> none  [the longest x8 11.7 us: on_device(): pieces.append(jnp.dot(matrix, window, preferred_element_type=jnp.float32))]
    slice x5 -> x0, local copies, waits for them, and re-layouts: 10.7 us -> none  [the longest x1 9.3 us: on_device(): matrix = jnp.where(same, skewed[number], jnp.zeros_like(skewed[number]))]
    ppermute x2 -> x0, starting transfers between devices: 6.5 us -> none  [the longest x1 4.58 us: with_halo(): lax.ppermute(tail, axis, [(i, (i + 1) % count) for i in range(ends)])]
    squeeze x8 -> x0, local copies, waits for them, and re-layouts: 3.75 us -> none  [on_device(): matrix = jnp.where(same, skewed[number], jnp.zeros_like(skewed[number]))]
    reshape x2 -> x0, local copies, waits for them, and re-layouts: 2.63 us -> none  [the longest x1 1.38 us: on_device(): widened.reshape(tiles, tile * (extent + 1))[:, :tile * extent]]
    unnamed x14 -> x1, local copies, waits for them, and re-layouts: 3.15 us -> 1.29 us
  transfers between devices with their start and end apart: 2 -> 0, of which waited for: 0 -> 0; matrix products, arithmetic and copies ran while one was open for 38% -> 0% of each run, Pallas kernels for 0% -> 0%
where the time goes in v1:
time: 39.4 us; the launch traced here: 39.2 us
  Pallas kernels  35.7 us (91%)
  local copies, waits for them, and re-layouts  2.79 us (7%)
  between operations  0.64 us (2%)
    pallas_call x1, Pallas kernels, on_device(): pl.pallas_call(kernel, out_shape=(jax.ShapeDtypeStruct((PRED * PRED, owne...  35.7 us
    pallas_call x1, local copies, waits for them, and re-layouts, on_device(): pl.pallas_call(kernel, out_shape=(jax.ShapeDtypeStruct((PRED * PRED, owne...  1.49 us
    unnamed x1, local copies, waits for them, and re-layouts  1.29 us

profile of v1, /device:TPU:1, one launch (start us, length us, event | category | flops | bytes accessed | tf_op | source)
XLA Modules:
  0.0 39.2 jit_solution(1841510801249920122)
XLA Ops:
  0.6 35.7 %normal_equations.1 = (f32[100,32]{1,0:T(8,128)}, f32[10,32]{1,0:T(8,128)}) custom-call(bf16[2048,2048]{1,0:T(8,128)(2,1)} %dep_ref.1, bf16[10,2048]{1,0:T(8,128)(2,1)} %pred_ref.1, bf16[63,2048]{1,0:T(8,128)(2,1)} %inv_ref.1, s32[64,128]{1,0:T(8,128)} %bitcast.1, s32[16]{0:T(128)} %lines_ref.1, bf16[16,512]{1,0:T(8,128)(2,1)} %constant.2.clone.sel_ref), custom_call_target="tpu_custom_call" | custom-call | tf_op jit(solution)/shard_map/normal_equations/pallas_call | solution.py:287
  36.4 1.5 %copy.8 = f32[100,32]{0,1:T(8,128)} copy(f32[100,32]{1,0:T(8,128)} %get-tuple-element.2) | data formatting | bytes 25600 | tf_op jit(solution)/shard_map/normal_equations/pallas_call | solution.py:287
  37.9 1.3 %copy.10 = f32[10,32]{1,0:T(8,128)} copy(f32[10,32]{1,0:T(8,128)} %get-tuple-element.7) | data formatting | bytes 2560

commit v2 on v1

--- a/solution.py
+++ b/solution.py
@@ -32,49 +32,77 @@
 
 
 def kernel(
-    dep_ref, pred_ref, inv_ref, ids_ref, lines_ref, sel_ref,
+    dep_ref, pred_hbm, inv_hbm, ids_hbm, lines_hbm, sel_hbm,
     gram_ref, rhs_ref,
-    cells, wq, ws, inv_t, id_rows, id_cols, send1, recv1, own, send2, recv2,
-    load_sem, halo_send, halo_recv, send1_sem, recv1_sem, send2_sem, recv2_sem,
+    cells, pred_ref, inv_ref, ids_ref, lines_ref, sel_ref,
+    wq, ws, id_rows, id_cols, mat_a, mat_b, weight0, scaled0,
+    send1, recv1, own, send2, recv2,
+    small_sem, load_sem, halo_send, halo_recv, send1_sem, recv1_sem, send2_sem, recv2_sem,
 ):
     obs = lax.axis_index("obs")
     chan = lax.axis_index("chan")
     z, p = obs // 8, obs % 8
     rows = dep_ref.shape[0]
     blocks = rows // BLOCK
+    parts = cells.shape[1] // 256
     factor = 1.0 / float(dep_ref.shape[1] * lax.axis_size("obs"))
     last = lax.axis_size("chan") - 1
     turn = 1 - 2 * (z // 4)
 
-    def block_at(step):
-        return (z + turn * (step + 1) + 2 * blocks) % blocks
-
-    def load(number):
+    barrier = pltpu.get_barrier_semaphore()
+
+    @pl.when(chan > 0)
+    def _():
+        pl.semaphore_signal(barrier, inc=1, device_id=(obs, chan - 1), device_id_type=MESH)
+
+    @pl.when(chan < last)
+    def _():
+        pl.semaphore_signal(barrier, inc=1, device_id=(obs, chan + 1), device_id_type=MESH)
+
+    smalls = [
+        pltpu.make_async_copy(source, target, small_sem.at[n])
+        for n, (source, target) in enumerate(
+            [
+                (pred_hbm, pred_ref),
+                (lines_hbm, lines_ref),
+                (sel_hbm, sel_ref),
+                (ids_hbm, ids_ref),
+                (inv_hbm, inv_ref),
+            ]
+        )
+    ]
+    for copy in smalls:
+        copy.start()
+
+    def piece(order):
+        return (z + turn * order + 2 * blocks) % blocks
+
+    def load(order):
+        number = piece(order)
         at = pl.multiple_of(number * BLOCK, BLOCK)
         return pltpu.make_async_copy(
             dep_ref.at[pl.ds(at, BLOCK)],
             cells.at[pl.ds(pl.multiple_of(at + HALO, HALO), BLOCK)],
-            load_sem.at[number],
-        )
-
-    def piece(order):
-        return (z + turn * order + 2 * blocks) % blocks
+            load_sem.at[order],
+        )
 
     for order in range(blocks):
-        load(piece(order)).start()
-
-    barrier = pltpu.get_barrier_semaphore()
+        load(order).start()
+
     for d in range(1, 8):
         pl.semaphore_signal(barrier, inc=1, device_id=((z + d) % 8 * 8 + p, chan), device_id_type=MESH)
         pl.semaphore_signal(barrier, inc=1, device_id=(z * 8 + (p + d) % 8, chan), device_id_type=MESH)
 
-    @pl.when(chan > 0)
-    def _():
-        pl.semaphore_signal(barrier, inc=1, device_id=(obs, chan - 1), device_id_type=MESH)
-
-    @pl.when(chan < last)
-    def _():
-        pl.semaphore_signal(barrier, inc=1, device_id=(obs, chan + 1), device_id_type=MESH)
+    @pl.when(chan == 0)
+    def _():
+        cells[pl.ds(0, HALO), :] = jnp.zeros((HALO, cells.shape[1]), jnp.bfloat16)
+
+    @pl.when(chan == last)
+    def _():
+        cells[pl.ds(HALO + rows, HALO), :] = jnp.zeros((HALO, cells.shape[1]), jnp.bfloat16)
+
+    for copy in smalls:
+        copy.wait()
 
     here = pl.multiple_of(chan * 16, 16)
     id_rows[pl.ds(8, 16), :] = ids_ref[pl.ds(here, 16), :].astype(jnp.float32)
@@ -87,27 +115,60 @@
     id_cols[:, 0:128] = jnp.where(lane16 < 32, turned[0], turned[1])
     id_cols[:, 128:256] = jnp.where(lane16 < 32, turned[1], turned[2])
 
-    @pl.loop(0, 16)
-    def _(s):
-        at = pl.multiple_of(s * 128, 128)
-        entries = inv_ref[:, pl.ds(at, 128)].astype(jnp.float32)
-        number = jnp.broadcast_to(id_rows[pl.ds(8 + s, 1), :], (64, 128))
-        stacked = jnp.concatenate([entries, jnp.zeros((1, 128), jnp.float32), number], axis=0)
-        inv_t[pl.ds(at, 128), :] = stacked.T
-
-    @pl.loop(0, 16)
-    def _(s):
-        at = pl.multiple_of(s * 128, 128)
+    for s in range(cells.shape[1] // 128):
         lane = lax.broadcasted_iota(jnp.int32, (PRED, 128), 1)
-        values = pred_ref[:, pl.ds(at, 128)].astype(jnp.float32)
+        values = pred_ref[:, s * 128 : s * 128 + 128].astype(jnp.float32)
         values = jnp.where(lane < lines_ref[s], values, 0.0)
         values = jnp.concatenate([values, jnp.zeros((16 - PRED, 128), jnp.float32)], axis=0)
         picked = jnp.dot(
             values.T.astype(jnp.bfloat16), sel_ref[...], preferred_element_type=jnp.float32
         )
         products = (picked[:, 0:128] * picked[:, 128:256]).astype(jnp.bfloat16)
-        wq[pl.ds(at, 128), :] = jnp.concatenate([products, jnp.zeros_like(products)], axis=1)
-        ws[pl.ds(at, 128), :] = picked[:, 256:512].astype(jnp.bfloat16)
+        wq[pl.ds(s * 128, 128), :] = jnp.concatenate([products, jnp.zeros_like(products)], axis=1)
+        ws[pl.ds(s * 128, 128), :] = picked[:, 256:512].astype(jnp.bfloat16)
+
+    def band(first):
+        block = first // 128
+        entries = inv_ref[:, pl.ds(first, 128)].astype(jnp.float32)
+        number = jnp.broadcast_to(id_rows[pl.ds(8 + block, 1), :], (64, 128))
+        both = jnp.concatenate([entries, jnp.zeros((1, 128), jnp.float32), number], axis=0).T
+        lane = lax.broadcasted_iota(jnp.int32, (128, 128), 1)
+        entries = jnp.where(lane < 64, both, 0.0)
+        number = jnp.where(lane < 64, pltpu.roll(both, 64, axis=1), both)
+        wide = jnp.concatenate([entries, jnp.zeros_like(entries)], axis=1)
+        wide = pltpu.roll(wide, 1, axis=1, stride=1, stride_axis=0)
+        near = id_cols[pl.ds(block, 1), :]
+        same = jnp.concatenate([number, number], axis=1) == near
+        return jnp.where(same, wide, 0.0).astype(jnp.bfloat16)
+
+    def start_of(number):
+        return pl.multiple_of(number * BLOCK, BLOCK)
+
+    def make(number, mat):
+        for n in range(2):
+            mat[n] = band(pl.multiple_of(start_of(number) + 128 * n, 128))
+
+    def product(number, mat, part):
+        first = start_of(number)
+        cols = pl.ds(part * 256, 256)
+        return [
+            jnp.dot(
+                mat[n][:, 0:WINDOW],
+                cells[pl.ds(pl.multiple_of(first + 128 * n, 128), WINDOW), cols],
+                preferred_element_type=jnp.float32,
+            )
+            for n in range(2)
+        ]
+
+    def weigh(weighted):
+        weight = [(1.0 / jnp.maximum(jnp.abs(w), 1.0)).astype(jnp.bfloat16) for w in weighted]
+        scaled = [jnp.clip(w, -1.0, 1.0).astype(jnp.bfloat16) for w in weighted]
+        return jnp.concatenate(weight, axis=0), jnp.concatenate(scaled, axis=0)
+
+    for order in range(3):
+        load(order).wait()
+    make(piece(1), mat_a)
+    weight0[...], scaled0[...] = weigh(product(piece(1), mat_a, 0))
 
     pl.semaphore_wait(barrier, 14 + jnp.minimum(chan, 1) + jnp.minimum(last - chan, 1))
 
@@ -139,14 +200,6 @@
     def _():
         down().start()
 
-    @pl.when(chan == 0)
-    def _():
-        cells[pl.ds(0, HALO), :] = jnp.zeros((HALO, cells.shape[1]), jnp.bfloat16)
-
-    @pl.when(chan == last)
-    def _():
-        cells[pl.ds(HALO + rows, HALO), :] = jnp.zeros((HALO, cells.shape[1]), jnp.bfloat16)
-
     def to_plane(number):
         return pltpu.make_async_remote_copy(
             src_ref=send1.at[number],
@@ -157,56 +210,34 @@
             device_id_type=MESH,
         )
 
-    def band(first):
-        lane = lax.broadcasted_iota(jnp.int32, (128, 128), 1)
-        both = inv_t[pl.ds(first, 128), :]
-        entries = jnp.where(lane < 64, both, 0.0)
-        number = jnp.where(lane < 64, pltpu.roll(both, 64, axis=1), both)
-        wide = jnp.concatenate([entries, jnp.zeros_like(entries)], axis=1)
-        wide = pltpu.roll(wide, 1, axis=1, stride=1, stride_axis=0)
-        near = id_cols[pl.ds(first // 128, 1), :]
-        same = jnp.concatenate([number, number], axis=1) == near
-        return jnp.where(same, wide, 0.0).astype(jnp.bfloat16)[:, 0:WINDOW]
-
-    load(piece(0)).wait()
-    load(piece(1)).wait()
-
-    @pl.loop(0, blocks)
-    def _(step):
-        number = block_at(step)
-
-        @pl.when(step < blocks - 2)
+    def block_step(step, mat, mat_next):
+        number, following = piece(step + 1), piece(step + 2)
+
+        @pl.when(step < blocks - 3)
         def _():
-            load(piece(step + 2)).wait()
-
-        @pl.when((number == 0) & (chan > 0))
+            load(step + 3).wait()
+
+        @pl.when((following == 0) & (chan > 0))
         def _():
             down().wait_recv()
 
-        @pl.when((number == blocks - 1) & (chan < last))
+        @pl.when((following == blocks - 1) & (chan < last))
         def _():
             up().wait_recv()
 
-        first = pl.multiple_of(number * BLOCK, BLOCK)
-        matrices = [band(first + 128 * n) for n in range(2)]
+        make(following, mat_next)
         total = jnp.zeros((BLOCK, 256), jnp.float32)
-        for part in range(cells.shape[1] // 256):
+        weight, scaled = weight0[...], scaled0[...]
+        for part in range(parts):
+            if part < parts - 1:
+                coming = product(number, mat, part + 1)
+            else:
+                coming = product(following, mat_next, 0)
             cols = pl.ds(part * 256, 256)
-            weighted = jnp.concatenate(
-                [
-                    jnp.dot(
-                        matrices[n],
-                        cells[pl.ds(pl.multiple_of(first + 128 * n, 128), WINDOW), cols],
-                        preferred_element_type=jnp.float32,
-                    )
-                    for n in range(2)
-                ],
-                axis=0,
-            )
-            weight = (1.0 / jnp.maximum(jnp.abs(weighted), 1.0)).astype(jnp.bfloat16)
-            scaled = jnp.clip(weighted, -1.0, 1.0).astype(jnp.bfloat16)
             total = total + jnp.dot(weight, wq[cols, :], preferred_element_type=jnp.float32)
             total = total + jnp.dot(scaled, ws[cols, :], preferred_element_type=jnp.float32)
+            weight, scaled = weigh(coming)
+        weight0[...], scaled0[...] = weight, scaled
 
         lane = lax.broadcasted_iota(jnp.int32, (8, 16, 128), 2)
         halves = total[:, 0:128].reshape(8, 2, 16, 128)
@@ -224,6 +255,11 @@
         @pl.when(step < blocks - 1)
         def _():
             to_plane(number).start()
+
+    @pl.loop(0, blocks // 2)
+    def _(pair):
+        block_step(2 * pair, mat_a, mat_b)
+        block_step(2 * pair + 1, mat_b, mat_a)
 
     def wait_for(buffer, sem):
         pltpu.make_async_copy(buffer.at[pl.ds(0, 7)], buffer.at[pl.ds(0, 7)], sem).wait()
@@ -290,27 +326,29 @@
             jax.ShapeDtypeStruct((PRED * PRED, owned), jnp.float32),
             jax.ShapeDtypeStruct((PRED, owned), jnp.float32),
         ),
-        in_specs=[
-            pl.BlockSpec(memory_space=pltpu.HBM),
-            vmem,
-            vmem,
-            vmem,
-            pl.BlockSpec(memory_space=pltpu.SMEM),
-            vmem,
-        ],
+        in_specs=[pl.BlockSpec(memory_space=pltpu.HBM)] * 6,
         out_specs=(vmem, vmem),
         scratch_shapes=[
             pltpu.VMEM((rows + 2 * HALO, obs_dev), jnp.bfloat16),
+            pltpu.VMEM(predictors.shape, jnp.bfloat16),
+            pltpu.VMEM(inv_band.shape, jnp.bfloat16),
+            pltpu.VMEM((band_id.shape[0] // 128, 128), jnp.int32),
+            pltpu.SMEM(line_counts.shape, jnp.int32),
+            pltpu.VMEM((16, 512), jnp.bfloat16),
             pltpu.VMEM((obs_dev, 256), jnp.bfloat16),
             pltpu.VMEM((obs_dev, 256), jnp.bfloat16),
-            pltpu.VMEM((rows, 128), jnp.float32),
             pltpu.VMEM((32, 128), jnp.float32),
             pltpu.VMEM((16, 256), jnp.float32),
+            pltpu.VMEM((2, 128, 256), jnp.bfloat16),
+            pltpu.VMEM((2, 128, 256), jnp.bfloat16),
+            pltpu.VMEM((BLOCK, 256), jnp.bfloat16),
+            pltpu.VMEM((BLOCK, 256), jnp.bfloat16),
             pltpu.VMEM((8, 17, 8, 128), jnp.bfloat16),
             pltpu.VMEM((8, 17, 8, 128), jnp.bfloat16),
             pltpu.VMEM((17, 8, 128), jnp.float32),
             pltpu.VMEM((8, 3, 8, 128), jnp.float32),
             pltpu.VMEM((8, 3, 8, 128), jnp.float32),
+            pltpu.SemaphoreType.DMA((5,)),
             pltpu.SemaphoreType.DMA((8,)),
             pltpu.SemaphoreType.DMA((2,)),
             pltpu.SemaphoreType.DMA((2,)),

time: 39.4 us -> 35.1 us (0.89)
  Pallas kernels: 35.7 us -> 31.5 us
    pallas_call x1, Pallas kernels: 35.7 us -> 31.5 us  [on_device(): pl.pallas_call(kernel, out_shape=(jax.ShapeDtypeStruct((PRED * PRED, owne...]
where the time goes in v2:
time: 35.1 us; the launch traced here: 34.9 us
  Pallas kernels  31.5 us (90%)
  local copies, waits for them, and re-layouts  2.79 us (8%)
  between operations  0.64 us (2%)
    pallas_call x1, Pallas kernels, on_device(): pl.pallas_call(kernel, out_shape=(jax.ShapeDtypeStruct((PRED * PRED, owne...  31.5 us
    pallas_call x1, local copies, waits for them, and re-layouts, on_device(): pl.pallas_call(kernel, out_shape=(jax.ShapeDtypeStruct((PRED * PRED, owne...  1.49 us
    unnamed x1, local copies, waits for them, and re-layouts  1.29 us

profile of v2, /device:TPU:1, one launch (start us, length us, event | category | flops | bytes accessed | tf_op | source)
XLA Modules:
  0.0 34.9 jit_solution(16753764433798700759)
XLA Ops:
  0.6 31.5 %normal_equations.1 = (f32[100,32]{1,0:T(8,128)}, f32[10,32]{1,0:T(8,128)}) custom-call(bf16[2048,2048]{1,0:T(8,128)(2,1)} %dep_ref.1, bf16[10,2048]{1,0:T(8,128)(2,1)} %pred_hbm.1, bf16[63,2048]{1,0:T(8,128)(2,1)} %inv_hbm.1, s32[64,128]{1,0:T(8,128)} %bitcast.1, s32[16]{0:T(128)} %lines_hbm.1, bf16[16,512]{1,0:T(8,128)(2,1)} %constant.2.clone.sel_hbm), custom_call_target="tpu_custom_call" | custom-call | tf_op jit(solution)/shard_map/normal_equations/pallas_call | solution.py:323
  32.2 1.5 %copy.8 = f32[100,32]{0,1:T(8,128)} copy(f32[100,32]{1,0:T(8,128)} %get-tuple-element.2) | data formatting | bytes 25600 | tf_op jit(solution)/shard_map/normal_equations/pallas_call | solution.py:323
  33.6 1.3 %copy.10 = f32[10,32]{1,0:T(8,128)} copy(f32[10,32]{1,0:T(8,128)} %get-tuple-element.7) | data formatting | bytes 2560

commit v3 on v2

--- a/solution.py
+++ b/solution.py
@@ -14,28 +14,56 @@
 BLOCK = 256
 WINDOW = 192
 PAIRS = [(j, k) for j in range(PRED) for k in range(j, PRED)]
-MAIN = 64
+HALF = 64
+TILES = 19
+
+ORDERS = (
+    (5, 6, 2, 1, 7, 3, 4, 0),
+    (5, 2, 6, 7, 3, 0, 4, 1),
+    (5, 6, 4, 0, 7, 1, 3, 2),
+    (2, 6, 1, 4, 7, 5, 0, 3),
+    (3, 2, 1, 7, 0, 6, 5, 4),
+    (1, 4, 2, 6, 0, 3, 7, 5),
+    (1, 5, 2, 0, 3, 7, 4, 6),
+    (4, 1, 3, 0, 6, 5, 2, 7),
+)
+
+
+def loads_of(order):
+    needed = []
+    for block in order:
+        for near in (block - 1, block, block + 1):
+            if 0 <= near < len(order) and near not in needed:
+                needed.append(near)
+    return tuple(needed)
+
+
+def code_of(order):
+    return sum(block * 8**n for n, block in enumerate(order))
+
+
+def pick(z, codes):
+    code = jnp.int32(codes[0])
+    for n in range(1, len(codes)):
+        code = jnp.where(z == n, jnp.int32(codes[n]), code)
+    return code
 
 
 def selectors():
     left = np.zeros((16, 128), np.float32)
     right = np.zeros((16, 128), np.float32)
-    alone = np.zeros((16, 256), np.float32)
     for half in range(2):
         for m, (j, k) in enumerate(PAIRS):
-            left[j, half * MAIN + m] = 1
-            right[k, half * MAIN + m] = 1
-        for k in range(PRED - 1):
-            alone[k, half * MAIN + len(PAIRS) + k] = 1
-    alone[PRED - 1, 128:] = 1
-    return np.concatenate([left, right, alone], axis=1)
+            left[j, half * HALF + m] = 1
+            right[k, half * HALF + m] = 1
+    return np.concatenate([left, right], axis=1)
 
 
 def kernel(
     dep_ref, pred_hbm, inv_hbm, ids_hbm, lines_hbm, sel_hbm,
     gram_ref, rhs_ref,
     cells, pred_ref, inv_ref, ids_ref, lines_ref, sel_ref,
-    wq, ws, id_rows, id_cols, mat_a, mat_b, weight0, scaled0,
+    wq, live_pred, id_rows, id_cols, mat_a, mat_b, weight0, scaled0,
     send1, recv1, own, send2, recv2,
     small_sem, load_sem, halo_send, halo_recv, send1_sem, recv1_sem, send2_sem, recv2_sem,
 ):
@@ -47,7 +75,8 @@
     parts = cells.shape[1] // 256
     factor = 1.0 / float(dep_ref.shape[1] * lax.axis_size("obs"))
     last = lax.axis_size("chan") - 1
-    turn = 1 - 2 * (z // 4)
+    order_code = pick(z, [code_of(order + order[:1]) for order in ORDERS])
+    load_code = pick(z, [code_of(loads_of(order)) for order in ORDERS])
 
     barrier = pltpu.get_barrier_semaphore()
 
@@ -74,11 +103,8 @@
     for copy in smalls:
         copy.start()
 
-    def piece(order):
-        return (z + turn * order + 2 * blocks) % blocks
-
     def load(order):
-        number = piece(order)
+        number = load_code // 8**order % 8
         at = pl.multiple_of(number * BLOCK, BLOCK)
         return pltpu.make_async_copy(
             dep_ref.at[pl.ds(at, BLOCK)],
@@ -120,12 +146,12 @@
         values = pred_ref[:, s * 128 : s * 128 + 128].astype(jnp.float32)
         values = jnp.where(lane < lines_ref[s], values, 0.0)
         values = jnp.concatenate([values, jnp.zeros((16 - PRED, 128), jnp.float32)], axis=0)
+        live_pred[:, s * 128 : s * 128 + 128] = values.astype(jnp.bfloat16)
         picked = jnp.dot(
             values.T.astype(jnp.bfloat16), sel_ref[...], preferred_element_type=jnp.float32
         )
         products = (picked[:, 0:128] * picked[:, 128:256]).astype(jnp.bfloat16)
         wq[pl.ds(s * 128, 128), :] = jnp.concatenate([products, jnp.zeros_like(products)], axis=1)
-        ws[pl.ds(s * 128, 128), :] = picked[:, 256:512].astype(jnp.bfloat16)
 
     def band(first):
         block = first // 128
@@ -167,8 +193,8 @@
 
     for order in range(3):
         load(order).wait()
-    make(piece(1), mat_a)
-    weight0[...], scaled0[...] = weigh(product(piece(1), mat_a, 0))
+    make(order_code % 8, mat_a)
+    weight0[...], scaled0[...] = weigh(product(order_code % 8, mat_a, 0))
 
     pl.semaphore_wait(barrier, 14 + jnp.minimum(chan, 1) + jnp.minimum(last - chan, 1))
 
@@ -210,12 +236,14 @@
             device_id_type=MESH,
         )
 
-    def block_step(step, mat, mat_next):
-        number, following = piece(step + 1), piece(step + 2)
-
-        @pl.when(step < blocks - 3)
-        def _():
-            load(step + 3).wait()
+    def block_step(step, number, following, mat, mat_next):
+
+        for start in range(2):
+
+            @pl.when(step == start)
+            def _(start=start):
+                for order in range(3 + 3 * start, min(6 + 3 * start, blocks)):
+                    load(order).wait()
 
         @pl.when((following == 0) & (chan > 0))
         def _():
@@ -227,6 +255,7 @@
 
         make(following, mat_next)
         total = jnp.zeros((BLOCK, 256), jnp.float32)
+        sides = jnp.zeros((16, BLOCK), jnp.float32)
         weight, scaled = weight0[...], scaled0[...]
         for part in range(parts):
             if part < parts - 1:
@@ -235,31 +264,33 @@
                 coming = product(following, mat_next, 0)
             cols = pl.ds(part * 256, 256)
             total = total + jnp.dot(weight, wq[cols, :], preferred_element_type=jnp.float32)
-            total = total + jnp.dot(scaled, ws[cols, :], preferred_element_type=jnp.float32)
+            sides = sides + lax.dot_general(
+                live_pred[:, cols], scaled, (((1,), (1,)), ((), ())), preferred_element_type=jnp.float32
+            )
             weight, scaled = weigh(coming)
         weight0[...], scaled0[...] = weight, scaled
 
         lane = lax.broadcasted_iota(jnp.int32, (8, 16, 128), 2)
         halves = total[:, 0:128].reshape(8, 2, 16, 128)
-        main = jnp.where(lane < MAIN, halves[:, 0], halves[:, 1]).reshape(16, 8, 128)
-        tenth = total[:, 128:256].reshape(8, 32, 128)
-        on = lax.broadcasted_iota(jnp.int32, (8, 32, 128), 2) == lax.broadcasted_iota(
-            jnp.int32, (8, 32, 128), 1
-        )
-        tenth = jnp.sum(jnp.where(on, tenth, 0.0), axis=1)
+        main = jnp.where(lane < HALF, halves[:, 0], halves[:, 1]).reshape(16, 8, 128)
         own[0:16] = main
-        own[16] = tenth
         send1[number, 0:16] = main.astype(jnp.bfloat16)
-        send1[number, 16] = tenth.astype(jnp.bfloat16)
+        rest = jnp.concatenate([sides[8:10, 0:128], sides[8:10, 128:256], jnp.zeros((4, 128), jnp.float32)], axis=0)
+        for n, tile in enumerate((sides[0:8, 0:128], sides[0:8, 128:256], rest)):
+            own[16 + n] = tile
+            send1[number, 16 + n] = tile.astype(jnp.bfloat16)
 
         @pl.when(step < blocks - 1)
         def _():
             to_plane(number).start()
 
-    @pl.loop(0, blocks // 2)
-    def _(pair):
-        block_step(2 * pair, mat_a, mat_b)
-        block_step(2 * pair + 1, mat_b, mat_a)
+    def pair(n, code):
+        first, second, third = code % 8, code // 8 % 8, code // 64 % 8
+        block_step(2 * n, first, second, mat_a, mat_b)
+        block_step(2 * n + 1, second, third, mat_b, mat_a)
+        return code // 64
+
+    lax.fori_loop(0, blocks // 2, pair, order_code)
 
     def wait_for(buffer, sem):
         pltpu.make_async_copy(buffer.at[pl.ds(0, 7)], buffer.at[pl.ds(0, 7)], sem).wait()
@@ -271,7 +302,9 @@
         sums = sums + jnp.where(source == z, jnp.zeros_like(came), came)
     for peer in range(8):
         send2[peer, 0:2] = sums[2 * peer : 2 * peer + 2]
-        send2[peer, 2] = sums[16]
+        at = peer % 4 * 32
+        low, high = sums[16 + peer // 4][:, at : at + 32], sums[18][:, at : at + 32]
+        send2[peer, 2] = jnp.concatenate([low, high, jnp.zeros((8, 64), jnp.float32)], axis=1)
 
     @pl.loop(1, 8)
     def _(d):
@@ -293,16 +326,15 @@
         whole = whole + jnp.where(source == p, jnp.zeros_like(came), came)
     whole = whole * factor
     flat = whole[0:2].reshape(16, 128).T
-    values = jnp.concatenate([flat[0:MAIN], flat[MAIN:128]], axis=1)
+    values = jnp.concatenate([flat[0:HALF], flat[HALF:128]], axis=1)
     index = {pair: m for m, pair in enumerate(PAIRS)}
     for j in range(PRED):
         for k in range(PRED):
             m = index[(min(j, k), max(j, k))]
             gram_ref[pl.ds(j * PRED + k, 1), :] = values[m : m + 1, :]
-    rhs_ref[0 : PRED - 1, :] = values[len(PAIRS) : MAIN, :]
-    row = lax.broadcasted_iota(jnp.int32, (8, 128), 0)
-    tenth = jnp.sum(jnp.where(row == p, whole[2], 0.0), axis=0, keepdims=True)
-    rhs_ref[PRED - 1 : PRED, :] = tenth[:, 0:32]
+    rhs_ref[0:8, :] = whole[2][:, 0:32]
+    rest = whole[2][:, 32:64]
+    rhs_ref[8:PRED, :] = jnp.where(p < 4, rest[0:2, :], rest[2:4, :])
 
     wait_for(send1, send1_sem)
     wait_for(send2, send2_sem)
@@ -334,18 +366,18 @@
             pltpu.VMEM(inv_band.shape, jnp.bfloat16),
             pltpu.VMEM((band_id.shape[0] // 128, 128), jnp.int32),
             pltpu.SMEM(line_counts.shape, jnp.int32),
-            pltpu.VMEM((16, 512), jnp.bfloat16),
+            pltpu.VMEM((16, 256), jnp.bfloat16),
             pltpu.VMEM((obs_dev, 256), jnp.bfloat16),
-            pltpu.VMEM((obs_dev, 256), jnp.bfloat16),
+            pltpu.VMEM((16, obs_dev), jnp.bfloat16),
             pltpu.VMEM((32, 128), jnp.float32),
             pltpu.VMEM((16, 256), jnp.float32),
             pltpu.VMEM((2, 128, 256), jnp.bfloat16),
             pltpu.VMEM((2, 128, 256), jnp.bfloat16),
             pltpu.VMEM((BLOCK, 256), jnp.bfloat16),
             pltpu.VMEM((BLOCK, 256), jnp.bfloat16),
-            pltpu.VMEM((8, 17, 8, 128), jnp.bfloat16),
-            pltpu.VMEM((8, 17, 8, 128), jnp.bfloat16),
-            pltpu.VMEM((17, 8, 128), jnp.float32),
+            pltpu.VMEM((8, TILES, 8, 128), jnp.bfloat16),
+            pltpu.VMEM((8, TILES, 8, 128), jnp.bfloat16),
+            pltpu.VMEM((TILES, 8, 128), jnp.float32),
             pltpu.VMEM((8, 3, 8, 128), jnp.float32),
             pltpu.VMEM((8, 3, 8, 128), jnp.float32),
             pltpu.SemaphoreType.DMA((5,)),

time: 35.1 us -> 32.8 us (0.934)
  Pallas kernels: 31.5 us -> 29.2 us
    pallas_call x1, Pallas kernels: 31.5 us -> 29.2 us  [on_device(): pl.pallas_call(kernel, out_shape=(jax.ShapeDtypeStruct((PRED * PRED, owne...]
where the time goes in v3:
time: 32.8 us; the launch traced here: 32.7 us
  Pallas kernels  29.2 us (89%)
  local copies, waits for them, and re-layouts  2.79 us (9%)
  between operations  0.64 us (2%)
    pallas_call x1, Pallas kernels, on_device(): pl.pallas_call(kernel, out_shape=(jax.ShapeDtypeStruct((PRED * PRED, owne...  29.2 us
    pallas_call x1, local copies, waits for them, and re-layouts, on_device(): pl.pallas_call(kernel, out_shape=(jax.ShapeDtypeStruct((PRED * PRED, owne...  1.49 us
    unnamed x1, local copies, waits for them, and re-layouts  1.29 us

profile of v3, /device:TPU:1, one launch (start us, length us, event | category | flops | bytes accessed | tf_op | source)
XLA Modules:
  0.0 32.7 jit_solution(3796711589745369269)
XLA Ops:
  0.6 29.2 %normal_equations.1 = (f32[100,32]{1,0:T(8,128)}, f32[10,32]{1,0:T(8,128)}) custom-call(bf16[2048,2048]{1,0:T(8,128)(2,1)} %dep_ref.1, bf16[10,2048]{1,0:T(8,128)(2,1)} %pred_hbm.1, bf16[63,2048]{1,0:T(8,128)(2,1)} %inv_hbm.1, s32[64,128]{1,0:T(8,128)} %bitcast.1, s32[16]{0:T(128)} %lines_hbm.1, bf16[16,256]{1,0:T(8,128)(2,1)} %constant.2.clone.sel_hbm), custom_call_target="tpu_custom_call" | custom-call | tf_op jit(solution)/shard_map/normal_equations/pallas_call | solution.py:355
  29.9 1.5 %copy.8 = f32[100,32]{0,1:T(8,128)} copy(f32[100,32]{1,0:T(8,128)} %get-tuple-element.2) | data formatting | bytes 25600 | tf_op jit(solution)/shard_map/normal_equations/pallas_call | solution.py:355
  31.4 1.3 %copy.10 = f32[10,32]{1,0:T(8,128)} copy(f32[10,32]{1,0:T(8,128)} %get-tuple-element.7) | data formatting | bytes 2560

commit v4 on v3

--- a/solution.py
+++ b/solution.py
@@ -18,15 +18,16 @@
 TILES = 19
 
 ORDERS = (
-    (5, 6, 2, 1, 7, 3, 4, 0),
-    (5, 2, 6, 7, 3, 0, 4, 1),
-    (5, 6, 4, 0, 7, 1, 3, 2),
-    (2, 6, 1, 4, 7, 5, 0, 3),
-    (3, 2, 1, 7, 0, 6, 5, 4),
-    (1, 4, 2, 6, 0, 3, 7, 5),
-    (1, 5, 2, 0, 3, 7, 4, 6),
-    (4, 1, 3, 0, 6, 5, 2, 7),
+    (2, 5, 4, 3, 1, 6, 7, 0),
+    (5, 2, 3, 6, 4, 0, 7, 1),
+    (4, 5, 1, 6, 0, 3, 7, 2),
+    (1, 5, 6, 0, 2, 4, 7, 3),
+    (6, 1, 2, 0, 5, 3, 7, 4),
+    (1, 4, 2, 3, 0, 7, 6, 5),
+    (3, 1, 2, 5, 0, 4, 7, 6),
+    (2, 5, 1, 3, 4, 0, 6, 7),
 )
+FAR = (4,)
 
 
 def loads_of(order):
@@ -61,11 +62,12 @@
 
 def kernel(
     dep_ref, pred_hbm, inv_hbm, ids_hbm, lines_hbm, sel_hbm,
-    gram_ref, rhs_ref,
+    sum_ref,
     cells, pred_ref, inv_ref, ids_ref, lines_ref, sel_ref,
     wq, live_pred, id_rows, id_cols, mat_a, mat_b, weight0, scaled0,
-    send1, recv1, own, send2, recv2,
+    send1, recv1, own, send2, recv2, far_send, far_recv, far_own, far_sum,
     small_sem, load_sem, halo_send, halo_recv, send1_sem, recv1_sem, send2_sem, recv2_sem,
+    far_send_sem, far_recv_sem,
 ):
     obs = lax.axis_index("obs")
     chan = lax.axis_index("chan")
@@ -235,6 +237,13 @@
             device_id=(number * 8 + p, chan),
             device_id_type=MESH,
         )
+
+    def split(tiles, target):
+        for peer in range(8):
+            target[peer, 0:2] = tiles[2 * peer : 2 * peer + 2]
+            at = peer % 4 * 32
+            low, high = tiles[16 + peer // 4][:, at : at + 32], tiles[18][:, at : at + 32]
+            target[peer, 2] = jnp.concatenate([low, high, jnp.zeros((8, 64), jnp.float32)], axis=1)
 
     def block_step(step, number, following, mat, mat_next):
 
@@ -280,7 +289,30 @@
             own[16 + n] = tile
             send1[number, 16 + n] = tile.astype(jnp.bfloat16)
 
-        @pl.when(step < blocks - 1)
+        ahead = (number - z + blocks) % blocks
+        near = ahead > 0
+        for n, distance in enumerate(FAR):
+            near = near & (ahead != distance)
+
+            @pl.when(ahead == distance)
+            def _(n=n):
+                split(own[...], send2)
+                far_send[n] = send2[...].astype(jnp.bfloat16)
+                far_own[n] = send2[p]
+
+                @pl.loop(1, 8)
+                def _(d):
+                    peer = (p + d) % 8
+                    pltpu.make_async_remote_copy(
+                        src_ref=far_send.at[n, peer],
+                        dst_ref=far_recv.at[n, p],
+                        send_sem=far_send_sem.at[n],
+                        recv_sem=far_recv_sem.at[n],
+                        device_id=(z * 8 + peer, chan),
+                        device_id_type=MESH,
+                    ).start()
+
+        @pl.when(near)
         def _():
             to_plane(number).start()
 
@@ -292,19 +324,38 @@
 
     lax.fori_loop(0, blocks // 2, pair, order_code)
 
-    def wait_for(buffer, sem):
-        pltpu.make_async_copy(buffer.at[pl.ds(0, 7)], buffer.at[pl.ds(0, 7)], sem).wait()
-
-    wait_for(recv1, recv1_sem)
+    def wait_for(buffer, count, sem):
+        pltpu.make_async_copy(buffer.at[pl.ds(0, count)], buffer.at[pl.ds(0, count)], sem).wait()
+
+    def far_copy(n):
+        return pltpu.make_async_remote_copy(
+            src_ref=far_sum.at[n],
+            dst_ref=recv2.at[8 + n],
+            send_sem=send2_sem,
+            recv_sem=recv2_sem,
+            device_id=((z + FAR[n]) % 8 * 8 + p, chan),
+            device_id_type=MESH,
+        )
+
+    for n in range(len(FAR)):
+        wait_for(far_recv.at[n], 7, far_recv_sem.at[n])
+        chunk = far_own[n]
+        for source in range(8):
+            came = far_recv[n, source].astype(jnp.float32)
+            chunk = chunk + jnp.where(source == p, jnp.zeros_like(came), came)
+        far_sum[n] = chunk
+        far_copy(n).start()
+
+    wait_for(recv1, 7 - len(FAR), recv1_sem)
     sums = own[...]
     for source in range(8):
         came = recv1[source].astype(jnp.float32)
-        sums = sums + jnp.where(source == z, jnp.zeros_like(came), came)
-    for peer in range(8):
-        send2[peer, 0:2] = sums[2 * peer : 2 * peer + 2]
-        at = peer % 4 * 32
-        low, high = sums[16 + peer // 4][:, at : at + 32], sums[18][:, at : at + 32]
-        send2[peer, 2] = jnp.concatenate([low, high, jnp.zeros((8, 64), jnp.float32)], axis=1)
+        away = (z - source + 8) % 8
+        absent = away == 0
+        for distance in FAR:
+            absent = absent | (away == distance)
+        sums = sums + jnp.where(absent, jnp.zeros_like(came), came)
+    split(sums, send2)
 
     @pl.loop(1, 8)
     def _(d):
@@ -319,25 +370,24 @@
         ).start()
 
     mine = send2[p]
-    wait_for(recv2, recv2_sem)
+    wait_for(recv2, 7 + len(FAR), recv2_sem)
     whole = mine
     for source in range(8):
         came = recv2[source]
         whole = whole + jnp.where(source == p, jnp.zeros_like(came), came)
-    whole = whole * factor
-    flat = whole[0:2].reshape(16, 128).T
-    values = jnp.concatenate([flat[0:HALF], flat[HALF:128]], axis=1)
-    index = {pair: m for m, pair in enumerate(PAIRS)}
-    for j in range(PRED):
-        for k in range(PRED):
-            m = index[(min(j, k), max(j, k))]
-            gram_ref[pl.ds(j * PRED + k, 1), :] = values[m : m + 1, :]
-    rhs_ref[0:8, :] = whole[2][:, 0:32]
-    rest = whole[2][:, 32:64]
-    rhs_ref[8:PRED, :] = jnp.where(p < 4, rest[0:2, :], rest[2:4, :])
-
-    wait_for(send1, send1_sem)
-    wait_for(send2, send2_sem)
+    for n in range(len(FAR)):
+        whole = whole + recv2[8 + n]
+    rest = whole[2]
+    lane = lax.broadcasted_iota(jnp.int32, (8, 128), 1)
+    row = lax.broadcasted_iota(jnp.int32, (8, 128), 0)
+    moved = pltpu.roll(rest, 6, axis=0)
+    sum_ref[0:2] = whole[0:2] * factor
+    sum_ref[2] = jnp.where((lane >= 32) & (row < 2) & (p >= 4), moved, rest) * factor
+
+    wait_for(send1, 7 - len(FAR), send1_sem)
+    wait_for(recv2, 7 + len(FAR), send2_sem)
+    for n in range(len(FAR)):
+        wait_for(far_send.at[n], 7, far_send_sem.at[n])
 
     @pl.when(chan > 0)
     def _():
@@ -346,20 +396,33 @@
     @pl.when(chan < last)
     def _():
         down().wait_send()
+
+
+def unpack(sum_ref, gram_ref, rhs_ref):
+    pairs = sum_ref[0:2].reshape(16, 128)
+    pairs = jnp.concatenate([pairs, pltpu.roll(pairs, HALF, axis=1)], axis=0)
+    entry = lax.broadcasted_iota(jnp.int32, (32, 128), 1)
+    left = jnp.zeros_like(entry)
+    for n in range(1, PRED):
+        left = left + jnp.where(entry >= n * PRED, 1, 0)
+    right = entry - left * PRED
+    low, high = jnp.minimum(left, right), jnp.maximum(left, right)
+    column = jnp.where(entry < PRED * PRED, low * PRED - (low * (low + 1)) // 2 + high, 0)
+    spread = jnp.take_along_axis(pairs, column, axis=1, mode="promise_in_bounds")
+    gram_ref[...] = spread[:, 0 : PRED * PRED]
+    rhs_ref[0:8, :] = sum_ref[2][:, 0:32]
+    rhs_ref[8:PRED, :] = sum_ref[2][0 : PRED - 8, 32:64]
 
 
 def on_device(departures, predictors, inv_band, band_id, line_counts):
     rows, obs_dev = departures.shape
     owned = rows // lax.axis_size("obs")
     vmem = pl.BlockSpec(memory_space=pltpu.VMEM)
-    return pl.pallas_call(
+    sums = pl.pallas_call(
         kernel,
-        out_shape=(
-            jax.ShapeDtypeStruct((PRED * PRED, owned), jnp.float32),
-            jax.ShapeDtypeStruct((PRED, owned), jnp.float32),
-        ),
+        out_shape=pltpu.VMEM((3, 8, 128), jnp.float32),
         in_specs=[pl.BlockSpec(memory_space=pltpu.HBM)] * 6,
-        out_specs=(vmem, vmem),
+        out_specs=vmem,
         scratch_shapes=[
             pltpu.VMEM((rows + 2 * HALO, obs_dev), jnp.bfloat16),
             pltpu.VMEM(predictors.shape, jnp.bfloat16),
@@ -379,7 +442,11 @@
             pltpu.VMEM((8, TILES, 8, 128), jnp.bfloat16),
             pltpu.VMEM((TILES, 8, 128), jnp.float32),
             pltpu.VMEM((8, 3, 8, 128), jnp.float32),
-            pltpu.VMEM((8, 3, 8, 128), jnp.float32),
+            pltpu.VMEM((8 + len(FAR), 3, 8, 128), jnp.float32),
+            pltpu.VMEM((len(FAR), 8, 3, 8, 128), jnp.bfloat16),
+            pltpu.VMEM((len(FAR), 8, 3, 8, 128), jnp.bfloat16),
+            pltpu.VMEM((len(FAR), 3, 8, 128), jnp.float32),
+            pltpu.VMEM((len(FAR), 3, 8, 128), jnp.float32),
             pltpu.SemaphoreType.DMA((5,)),
             pltpu.SemaphoreType.DMA((8,)),
             pltpu.SemaphoreType.DMA((2,)),
@@ -388,6 +455,8 @@
             pltpu.SemaphoreType.DMA,
             pltpu.SemaphoreType.DMA,
             pltpu.SemaphoreType.DMA,
+            pltpu.SemaphoreType.DMA((len(FAR),)),
+            pltpu.SemaphoreType.DMA((len(FAR),)),
         ],
         compiler_params=pltpu.CompilerParams(collective_id=0, has_side_effects=True),
         name="normal_equations",
@@ -399,6 +468,17 @@
         line_counts,
         jnp.asarray(selectors(), jnp.bfloat16),
     )
+    gram, rhs = pl.pallas_call(
+        unpack,
+        out_shape=(
+            jax.ShapeDtypeStruct((owned, PRED * PRED), jnp.float32),
+            jax.ShapeDtypeStruct((PRED, owned), jnp.float32),
+        ),
+        in_specs=[vmem],
+        out_specs=(vmem, vmem),
+        name="unpack",
+    )(sums)
+    return gram.T, rhs
 
 
 def solution(mesh):

time: 32.8 us -> 29.6 us (0.902)
  local copies, waits for them, and re-layouts: 2.79 us -> 0.59 us
  Pallas kernels: 29.2 us -> 28.2 us
    pallas_call x1 -> x0, local copies, waits for them, and re-layouts: 1.49 us -> none  [on_device(): pl.pallas_call(kernel, out_shape=(jax.ShapeDtypeStruct((PRED * PRED, owne...]
    pallas_call x1 -> x2, Pallas kernels: 29.2 us -> 28.2 us  [the longest x1 26.8 us: on_device(): pl.pallas_call(kernel, out_shape=pltpu.VMEM((3, 8, 128), jnp.float32), in...]
    unnamed x1 -> x2, local copies, waits for them, and re-layouts: 1.29 us -> 0.59 us
where the time goes in v4:
time: 29.6 us; the launch traced here: 29.5 us
  Pallas kernels  28.2 us (95%)
  between operations  0.65 us (2%)
  local copies, waits for them, and re-layouts  0.59 us (2%)
    pallas_call x1, Pallas kernels, on_device(): pl.pallas_call(kernel, out_shape=pltpu.VMEM((3, 8, 128), jnp.float32), in...  26.8 us
    pallas_call x1, Pallas kernels, on_device(): pl.pallas_call(unpack, out_shape=(jax.ShapeDtypeStruct((owned, PRED * PRE...  1.45 us

profile of v4, /device:TPU:1, one launch (start us, length us, event | category | flops | bytes accessed | tf_op | source)
XLA Modules:
  0.0 29.5 jit_solution(6445533908640625300)
XLA Ops:
  0.6 26.8 %normal_equations.1.sum_ref = f32[3,8,128]{2,1,0:T(8,128)S(1)} custom-call(bf16[2048,2048]{1,0:T(8,128)(2,1)} %dep_ref.1, bf16[10,2048]{1,0:T(8,128)(2,1)} %pred_hbm.1, bf16[63,2048]{1,0:T(8,128)(2,1)} %inv_hbm.1, s32[64,128]{1,0:T(8,128)} %bitcast.2, s32[16]{0:T(128)} %lines_hbm.1, bf16[16,256]{1,0:T(8,128)(2,1)} %constant.2.clone.sel_hbm), custom_call_target="tpu_custom_call" | custom-call | tf_op jit(solution)/shard_map/normal_equations/pallas_call | solution.py:421
  27.4 0.0 copy-start
  27.4 0.6 %copy-done = f32[3,8,128]{2,1,0:T(8,128)} copy-done((f32[3,8,128]{2,1,0:T(8,128)}, f32[3,8,128]{2,1,0:T(8,128)S(1)}, u32[]{:S(2)}) %copy-start) | copy-done | bytes 12312
  28.0 1.5 %unpack.1 = (f32[32,100]{1,0:T(8,128)}, f32[10,32]{1,0:T(8,128)}) custom-call(f32[3,8,128]{2,1,0:T(8,128)} %copy-done), custom_call_target="tpu_custom_call" | custom-call | tf_op jit(solution)/shard_map/unpack/pallas_call | solution.py:471
Async XLA Ops:
  27.4 0.6 %copy-start = (f32[3,8,128]{2,1,0:T(8,128)}, f32[3,8,128]{2,1,0:T(8,128)S(1)}, u32[]{:S(2)}) copy-start(f32[3,8,128]{2,1,0:T(8,128)S(1)} %normal_equations.1.sum_ref) | copy-start | bytes 36868

commit v5 on v4

--- a/solution.py
+++ b/solution.py
@@ -63,12 +63,27 @@
 def kernel(
     dep_ref, pred_hbm, inv_hbm, ids_hbm, lines_hbm, sel_hbm,
     sum_ref,
-    cells, pred_ref, inv_ref, ids_ref, lines_ref, sel_ref,
+    cells, edges, pred_ref, inv_ref, ids_ref, lines_ref, sel_ref,
     wq, live_pred, id_rows, id_cols, mat_a, mat_b, weight0, scaled0,
     send1, recv1, own, send2, recv2, far_send, far_recv, far_own, far_sum,
-    small_sem, load_sem, halo_send, halo_recv, send1_sem, recv1_sem, send2_sem, recv2_sem,
+    small_sem, load_sem, edge_sem, halo_send, halo_recv, send1_sem, recv1_sem, send2_sem, recv2_sem,
     far_send_sem, far_recv_sem,
 ):
+    smalls = [
+        pltpu.make_async_copy(source, target, small_sem.at[n])
+        for n, (source, target) in enumerate(
+            [
+                (pred_hbm, pred_ref),
+                (lines_hbm, lines_ref),
+                (sel_hbm, sel_ref),
+                (ids_hbm, ids_ref),
+                (inv_hbm, inv_ref),
+            ]
+        )
+    ]
+    for copy in smalls:
+        copy.start()
+
     obs = lax.axis_index("obs")
     chan = lax.axis_index("chan")
     z, p = obs // 8, obs % 8
@@ -90,21 +105,6 @@
     def _():
         pl.semaphore_signal(barrier, inc=1, device_id=(obs, chan + 1), device_id_type=MESH)
 
-    smalls = [
-        pltpu.make_async_copy(source, target, small_sem.at[n])
-        for n, (source, target) in enumerate(
-            [
-                (pred_hbm, pred_ref),
-                (lines_hbm, lines_ref),
-                (sel_hbm, sel_ref),
-                (ids_hbm, ids_ref),
-                (inv_hbm, inv_ref),
-            ]
-        )
-    ]
-    for copy in smalls:
-        copy.start()
-
     def load(order):
         number = load_code // 8**order % 8
         at = pl.multiple_of(number * BLOCK, BLOCK)
@@ -114,8 +114,16 @@
             load_sem.at[order],
         )
 
+    def edge(n):
+        return pltpu.make_async_copy(
+            dep_ref.at[pl.ds(n * (rows - HALO), HALO)], edges.at[n], edge_sem.at[n]
+        )
+
     for order in range(blocks):
         load(order).start()
+        if order == 2:
+            for n in range(2):
+                edge(n).start()
 
     for d in range(1, 8):
         pl.semaphore_signal(barrier, inc=1, device_id=((z + d) % 8 * 8 + p, chan), device_id_type=MESH)
@@ -142,18 +150,6 @@
     turned = [pltpu.roll(id_rows[pl.ds(7 + n, 16), :], 32, axis=1) for n in range(3)]
     id_cols[:, 0:128] = jnp.where(lane16 < 32, turned[0], turned[1])
     id_cols[:, 128:256] = jnp.where(lane16 < 32, turned[1], turned[2])
-
-    for s in range(cells.shape[1] // 128):
-        lane = lax.broadcasted_iota(jnp.int32, (PRED, 128), 1)
-        values = pred_ref[:, s * 128 : s * 128 + 128].astype(jnp.float32)
-        values = jnp.where(lane < lines_ref[s], values, 0.0)
-        values = jnp.concatenate([values, jnp.zeros((16 - PRED, 128), jnp.float32)], axis=0)
-        live_pred[:, s * 128 : s * 128 + 128] = values.astype(jnp.bfloat16)
-        picked = jnp.dot(
-            values.T.astype(jnp.bfloat16), sel_ref[...], preferred_element_type=jnp.float32
-        )
-        products = (picked[:, 0:128] * picked[:, 128:256]).astype(jnp.bfloat16)
-        wq[pl.ds(s * 128, 128), :] = jnp.concatenate([products, jnp.zeros_like(products)], axis=1)
 
     def band(first):
         block = first // 128
@@ -176,6 +172,20 @@
         for n in range(2):
             mat[n] = band(pl.multiple_of(start_of(number) + 128 * n, 128))
 
+    make(order_code % 8, mat_a)
+
+    for s in range(cells.shape[1] // 128):
+        lane = lax.broadcasted_iota(jnp.int32, (PRED, 128), 1)
+        values = pred_ref[:, s * 128 : s * 128 + 128].astype(jnp.float32)
+        values = jnp.where(lane < lines_ref[s], values, 0.0)
+        values = jnp.concatenate([values, jnp.zeros((16 - PRED, 128), jnp.float32)], axis=0)
+        live_pred[:, s * 128 : s * 128 + 128] = values.astype(jnp.bfloat16)
+        picked = jnp.dot(
+            values.T.astype(jnp.bfloat16), sel_ref[...], preferred_element_type=jnp.float32
+        )
+        products = (picked[:, 0:128] * picked[:, 128:256]).astype(jnp.bfloat16)
+        wq[pl.ds(s * 128, 128), :] = jnp.concatenate([products, jnp.zeros_like(products)], axis=1)
+
     def product(number, mat, part):
         first = start_of(number)
         cols = pl.ds(part * 256, 256)
@@ -195,14 +205,13 @@
 
     for order in range(3):
         load(order).wait()
-    make(order_code % 8, mat_a)
     weight0[...], scaled0[...] = weigh(product(order_code % 8, mat_a, 0))
 
     pl.semaphore_wait(barrier, 14 + jnp.minimum(chan, 1) + jnp.minimum(last - chan, 1))
 
     def up():
         return pltpu.make_async_remote_copy(
-            src_ref=dep_ref.at[pl.ds(0, HALO)],
+            src_ref=edges.at[0],
             dst_ref=cells.at[pl.ds(HALO + rows, HALO)],
             send_sem=halo_send.at[0],
             recv_sem=halo_recv.at[0],
@@ -212,13 +221,16 @@
 
     def down():
         return pltpu.make_async_remote_copy(
-            src_ref=dep_ref.at[pl.ds(rows - HALO, HALO)],
+            src_ref=edges.at[1],
             dst_ref=cells.at[pl.ds(0, HALO)],
             send_sem=halo_send.at[1],
             recv_sem=halo_recv.at[1],
             device_id=(obs, jnp.minimum(chan + 1, last)),
             device_id_type=MESH,
         )
+
+    for n in range(2):
+        edge(n).wait()
 
     @pl.when(chan > 0)
     def _():
@@ -425,6 +437,7 @@
         out_specs=vmem,
         scratch_shapes=[
             pltpu.VMEM((rows + 2 * HALO, obs_dev), jnp.bfloat16),
+            pltpu.VMEM((2, HALO, obs_dev), jnp.bfloat16),
             pltpu.VMEM(predictors.shape, jnp.bfloat16),
             pltpu.VMEM(inv_band.shape, jnp.bfloat16),
             pltpu.VMEM((band_id.shape[0] // 128, 128), jnp.int32),
@@ -449,6 +462,7 @@
             pltpu.VMEM((len(FAR), 3, 8, 128), jnp.float32),
             pltpu.SemaphoreType.DMA((5,)),
             pltpu.SemaphoreType.DMA((8,)),
+            pltpu.SemaphoreType.DMA((2,)),
             pltpu.SemaphoreType.DMA((2,)),
             pltpu.SemaphoreType.DMA((2,)),
             pltpu.SemaphoreType.DMA,
@@ -477,7 +491,7 @@
         in_specs=[vmem],
         out_specs=(vmem, vmem),
         name="unpack",
-    )(sums)
+    )(pltpu.with_memory_space_constraint(sums, pltpu.VMEM))
     return gram.T, rhs
 
 

time: 29.6 us -> 27.7 us (0.936)
  Pallas kernels: 28.2 us -> 26.9 us
  local copies, waits for them, and re-layouts: 0.59 us -> 0 us
    pallas_call x1, Pallas kernels: 1.45 us -> 0.75 us  [on_device(): pl.pallas_call(unpack, out_shape=(jax.ShapeDtypeStruct((owned, PRED * PRE...]
    pallas_call x1, Pallas kernels: 26.8 us -> 26.1 us  [on_device(): pl.pallas_call(kernel, out_shape=pltpu.VMEM((3, 8, 128), jnp.float32), in...]
    unnamed x2 -> x0, local copies, waits for them, and re-layouts: 0.59 us -> none
where the time goes in v5:
time: 27.7 us; the launch traced here: 27.5 us
  Pallas kernels  26.9 us (97%)
  between operations  0.64 us (2%)
    pallas_call x1, Pallas kernels, on_device(): pl.pallas_call(kernel, out_shape=pltpu.VMEM((3, 8, 128), jnp.float32), in...  26.1 us
    pallas_call x1, Pallas kernels, on_device(): pl.pallas_call(unpack, out_shape=(jax.ShapeDtypeStruct((owned, PRED * PRE...  0.75 us

profile of v5, /device:TPU:1, one launch (start us, length us, event | category | flops | bytes accessed | tf_op | source)
XLA Modules:
  0.0 27.5 jit_solution(1266778795531977235)
XLA Ops:
  0.6 26.1 %normal_equations.1.sum_ref = f32[3,8,128]{2,1,0:T(8,128)S(1)} custom-call(bf16[2048,2048]{1,0:T(8,128)(2,1)} %dep_ref.1, bf16[10,2048]{1,0:T(8,128)(2,1)} %pred_hbm.1, bf16[63,2048]{1,0:T(8,128)(2,1)} %inv_hbm.1, s32[64,128]{1,0:T(8,128)} %bitcast.2, s32[16]{0:T(128)} %lines_hbm.1, bf16[16,256]{1,0:T(8,128)(2,1)} %constant.2.clone.sel_hbm), custom_call_target="tpu_custom_call" | custom-call | tf_op jit(solution)/shard_map/normal_equations/pallas_call | solution.py:433
  26.8 0.7 %unpack.1 = (f32[32,100]{1,0:T(8,128)}, f32[10,32]{1,0:T(8,128)}) custom-call(f32[3,8,128]{2,1,0:T(8,128)S(1)} %normal_equations.1.sum_ref), custom_call_target="tpu_custom_call" | custom-call | tf_op jit(solution)/shard_map/unpack/pallas_call | solution.py:485

commit v6 on v5

--- a/solution.py
+++ b/solution.py
@@ -66,8 +66,9 @@
     cells, edges, pred_ref, inv_ref, ids_ref, lines_ref, sel_ref,
     wq, live_pred, id_rows, id_cols, mat_a, mat_b, weight0, scaled0,
     send1, recv1, own, send2, recv2, far_send, far_recv, far_own, far_sum,
+    straight_send, straight_recv, ending,
     small_sem, load_sem, edge_sem, halo_send, halo_recv, send1_sem, recv1_sem, send2_sem, recv2_sem,
-    far_send_sem, far_recv_sem,
+    far_send_sem, far_recv_sem, straight_send_sem, straight_recv_sem,
 ):
     smalls = [
         pltpu.make_async_copy(source, target, small_sem.at[n])
@@ -128,6 +129,14 @@
     for d in range(1, 8):
         pl.semaphore_signal(barrier, inc=1, device_id=((z + d) % 8 * 8 + p, chan), device_id_type=MESH)
         pl.semaphore_signal(barrier, inc=1, device_id=(z * 8 + (p + d) % 8, chan), device_id_type=MESH)
+
+    @pl.when(z == 0)
+    def _():
+        for d in range(1, 8):
+            for upper in range(1, 8):
+                pl.semaphore_signal(
+                    barrier, inc=1, device_id=(upper * 8 + (p + d) % 8, chan), device_id_type=MESH
+                )
 
     @pl.when(chan == 0)
     def _():
@@ -207,7 +216,9 @@
         load(order).wait()
     weight0[...], scaled0[...] = weigh(product(order_code % 8, mat_a, 0))
 
-    pl.semaphore_wait(barrier, 14 + jnp.minimum(chan, 1) + jnp.minimum(last - chan, 1))
+    pl.semaphore_wait(
+        barrier, 14 + jnp.minimum(chan, 1) + jnp.minimum(last - chan, 1) + 7 * jnp.minimum(z, 1)
+    )
 
     def up():
         return pltpu.make_async_remote_copy(
@@ -302,11 +313,29 @@
             send1[number, 16 + n] = tile.astype(jnp.bfloat16)
 
         ahead = (number - z + blocks) % blocks
-        near = ahead > 0
+        straight = (number == 0) & (z > 0)
+        near = (ahead > 0) & jnp.logical_not(straight)
+
+        @pl.when(straight)
+        def _():
+            split(own[...], send2)
+            straight_send[...] = send2[...].astype(jnp.bfloat16)
+
+            @pl.loop(0, 8)
+            def _(owner):
+                pltpu.make_async_remote_copy(
+                    src_ref=straight_send.at[owner],
+                    dst_ref=straight_recv.at[(z - 1) * 8 + p],
+                    send_sem=straight_send_sem,
+                    recv_sem=straight_recv_sem,
+                    device_id=(owner, chan),
+                    device_id_type=MESH,
+                ).start()
+
         for n, distance in enumerate(FAR):
             near = near & (ahead != distance)
 
-            @pl.when(ahead == distance)
+            @pl.when((ahead == distance) & jnp.logical_not(straight))
             def _(n=n):
                 split(own[...], send2)
                 far_send[n] = send2[...].astype(jnp.bfloat16)
@@ -349,21 +378,26 @@
             device_id_type=MESH,
         )
 
-    for n in range(len(FAR)):
-        wait_for(far_recv.at[n], 7, far_recv_sem.at[n])
-        chunk = far_own[n]
-        for source in range(8):
-            came = far_recv[n, source].astype(jnp.float32)
-            chunk = chunk + jnp.where(source == p, jnp.zeros_like(came), came)
-        far_sum[n] = chunk
-        far_copy(n).start()
-
-    wait_for(recv1, 7 - len(FAR), recv1_sem)
+    @pl.when(z != 4)
+    def _():
+        for n in range(len(FAR)):
+            wait_for(far_recv.at[n], 7, far_recv_sem.at[n])
+            chunk = far_own[n]
+            for source in range(8):
+                came = far_recv[n, source].astype(jnp.float32)
+                chunk = chunk + jnp.where(source == p, jnp.zeros_like(came), came)
+            far_sum[n] = chunk
+            far_copy(n).start()
+
+    @pl.when(z > 0)
+    def _():
+        wait_for(recv1, 6, recv1_sem)
+
     sums = own[...]
     for source in range(8):
         came = recv1[source].astype(jnp.float32)
         away = (z - source + 8) % 8
-        absent = away == 0
+        absent = (away == 0) | (z == 0)
         for distance in FAR:
             absent = absent | (away == distance)
         sums = sums + jnp.where(absent, jnp.zeros_like(came), came)
@@ -382,13 +416,33 @@
         ).start()
 
     mine = send2[p]
-    wait_for(recv2, 7 + len(FAR), recv2_sem)
+    @pl.when(z == 0)
+    def _():
+        wait_for(recv2, 7, recv2_sem)
+
+    @pl.when(z > 0)
+    def _():
+        wait_for(recv2, 8, recv2_sem)
+
     whole = mine
     for source in range(8):
         came = recv2[source]
         whole = whole + jnp.where(source == p, jnp.zeros_like(came), came)
-    for n in range(len(FAR)):
-        whole = whole + recv2[8 + n]
+    ending[...] = whole
+
+    @pl.when(z > 0)
+    def _():
+        ending[...] = ending[...] + recv2[8]
+
+    @pl.when(z == 0)
+    def _():
+        wait_for(straight_recv, 56, straight_recv_sem)
+        more = ending[...]
+        for source in range(56):
+            more = more + straight_recv[source].astype(jnp.float32)
+        ending[...] = more
+
+    whole = ending[...]
     rest = whole[2]
     lane = lax.broadcasted_iota(jnp.int32, (8, 128), 1)
     row = lax.broadcasted_iota(jnp.int32, (8, 128), 0)
@@ -396,10 +450,26 @@
     sum_ref[0:2] = whole[0:2] * factor
     sum_ref[2] = jnp.where((lane >= 32) & (row < 2) & (p >= 4), moved, rest) * factor
 
-    wait_for(send1, 7 - len(FAR), send1_sem)
-    wait_for(recv2, 7 + len(FAR), send2_sem)
-    for n in range(len(FAR)):
-        wait_for(far_send.at[n], 7, far_send_sem.at[n])
+    @pl.when(z % 4 > 0)
+    def _():
+        wait_for(send1, 5, send1_sem)
+
+    @pl.when(z % 4 == 0)
+    def _():
+        wait_for(send1, 6, send1_sem)
+
+    @pl.when(z == 4)
+    def _():
+        wait_for(recv2, 7, send2_sem)
+
+    @pl.when(z != 4)
+    def _():
+        wait_for(recv2, 8, send2_sem)
+        wait_for(far_send.at[0], 7, far_send_sem.at[0])
+
+    @pl.when(z > 0)
+    def _():
+        wait_for(straight_send, 8, straight_send_sem)
 
     @pl.when(chan > 0)
     def _():
@@ -460,6 +530,9 @@
             pltpu.VMEM((len(FAR), 8, 3, 8, 128), jnp.bfloat16),
             pltpu.VMEM((len(FAR), 3, 8, 128), jnp.float32),
             pltpu.VMEM((len(FAR), 3, 8, 128), jnp.float32),
+            pltpu.VMEM((8, 3, 8, 128), jnp.bfloat16),
+            pltpu.VMEM((56, 3, 8, 128), jnp.bfloat16),
+            pltpu.VMEM((3, 8, 128), jnp.float32),
             pltpu.SemaphoreType.DMA((5,)),
             pltpu.SemaphoreType.DMA((8,)),
             pltpu.SemaphoreType.DMA((2,)),
@@ -471,6 +544,8 @@
             pltpu.SemaphoreType.DMA,
             pltpu.SemaphoreType.DMA((len(FAR),)),
             pltpu.SemaphoreType.DMA((len(FAR),)),
+            pltpu.SemaphoreType.DMA,
+            pltpu.SemaphoreType.DMA,
         ],
         compiler_params=pltpu.CompilerParams(collective_id=0, has_side_effects=True),
         name="normal_equations",

time: 27.7 us -> 27 us (0.975)
  Pallas kernels: 26.9 us -> 25.9 us
    pallas_call x1, Pallas kernels: 26.1 us -> 25.2 us  [on_device(): pl.pallas_call(kernel, out_shape=pltpu.VMEM((3, 8, 128), jnp.float32), in...]
where the time goes in v6:
time: 27 us; the launch traced here: 26.6 us
  Pallas kernels  25.9 us (96%)
  between operations  0.64 us (2%)
    pallas_call x1, Pallas kernels, on_device(): pl.pallas_call(kernel, out_shape=pltpu.VMEM((3, 8, 128), jnp.float32), in...  25.2 us
    pallas_call x1, Pallas kernels, on_device(): pl.pallas_call(unpack, out_shape=(jax.ShapeDtypeStruct((owned, PRED * PRE...  0.75 us

profile of v6, /device:TPU:1, one launch (start us, length us, event | category | flops | bytes accessed | tf_op | source)
XLA Modules:
  0.0 26.6 jit_solution(13037659286184649112)
XLA Ops:
  0.6 25.2 %normal_equations.1.sum_ref = f32[3,8,128]{2,1,0:T(8,128)S(1)} custom-call(bf16[2048,2048]{1,0:T(8,128)(2,1)} %dep_ref.1, bf16[10,2048]{1,0:T(8,128)(2,1)} %pred_hbm.1, bf16[63,2048]{1,0:T(8,128)(2,1)} %inv_hbm.1, s32[64,128]{1,0:T(8,128)} %bitcast.2, s32[16]{0:T(128)} %lines_hbm.1, bf16[16,256]{1,0:T(8,128)(2,1)} %constant.2.clone.sel_hbm), custom_call_target="tpu_custom_call" | custom-call | tf_op jit(solution)/shard_map/normal_equations/pallas_call | solution.py:503
  25.8 0.7 %unpack.1 = (f32[32,100]{1,0:T(8,128)}, f32[10,32]{1,0:T(8,128)}) custom-call(f32[3,8,128]{2,1,0:T(8,128)S(1)} %normal_equations.1.sum_ref), custom_call_target="tpu_custom_call" | custom-call | tf_op jit(solution)/shard_map/unpack/pallas_call | solution.py:560

commit v7 on v6

--- a/solution.py
+++ b/solution.py
@@ -19,13 +19,13 @@
 
 ORDERS = (
     (2, 5, 4, 3, 1, 6, 7, 0),
-    (5, 2, 3, 6, 4, 0, 7, 1),
-    (4, 5, 1, 6, 0, 3, 7, 2),
+    (5, 2, 3, 0, 6, 4, 7, 1),
+    (4, 5, 1, 0, 6, 3, 7, 2),
     (1, 5, 6, 0, 2, 4, 7, 3),
     (6, 1, 2, 0, 5, 3, 7, 4),
-    (1, 4, 2, 3, 0, 7, 6, 5),
-    (3, 1, 2, 5, 0, 4, 7, 6),
-    (2, 5, 1, 3, 4, 0, 6, 7),
+    (1, 4, 2, 0, 3, 7, 6, 5),
+    (3, 1, 2, 0, 5, 4, 7, 6),
+    (2, 5, 1, 0, 3, 4, 6, 7),
 )
 FAR = (4,)
 
@@ -195,6 +195,15 @@
         products = (picked[:, 0:128] * picked[:, 128:256]).astype(jnp.bfloat16)
         wq[pl.ds(s * 128, 128), :] = jnp.concatenate([products, jnp.zeros_like(products)], axis=1)
 
+    def one(number, mat, part, n):
+        return jnp.dot(
+            mat[n][:, 0:WINDOW],
+            cells[
+                pl.ds(pl.multiple_of(start_of(number) + 128 * n, 128), WINDOW), pl.ds(part * 256, 256)
+            ],
+            preferred_element_type=jnp.float32,
+        )
+
     def product(number, mat, part):
         first = start_of(number)
         cols = pl.ds(part * 256, 256)
@@ -290,15 +299,15 @@
         sides = jnp.zeros((16, BLOCK), jnp.float32)
         weight, scaled = weight0[...], scaled0[...]
         for part in range(parts):
-            if part < parts - 1:
-                coming = product(number, mat, part + 1)
-            else:
-                coming = product(following, mat_next, 0)
             cols = pl.ds(part * 256, 256)
-            total = total + jnp.dot(weight, wq[cols, :], preferred_element_type=jnp.float32)
+            at, block, using = (part + 1, number, mat) if part < parts - 1 else (0, following, mat_next)
+            coming = []
+            coming.append(one(block, using, at, 0))
+            coming.append(one(block, using, at, 1))
             sides = sides + lax.dot_general(
                 live_pred[:, cols], scaled, (((1,), (1,)), ((), ())), preferred_element_type=jnp.float32
             )
+            total = total + jnp.dot(weight, wq[cols, :], preferred_element_type=jnp.float32)
             weight, scaled = weigh(coming)
         weight0[...], scaled0[...] = weight, scaled
 

time: 27 us -> 26.1 us (0.967)
  Pallas kernels: 25.9 us -> 25.1 us
    pallas_call x1, Pallas kernels: 25.2 us -> 24.4 us  [on_device(): pl.pallas_call(kernel, out_shape=pltpu.VMEM((3, 8, 128), jnp.float32), in...]
where the time goes in v7:
time: 26.1 us; the launch traced here: 25.8 us
  Pallas kernels  25.1 us (96%)
  between operations  0.64 us (2%)
    pallas_call x1, Pallas kernels, on_device(): pl.pallas_call(kernel, out_shape=pltpu.VMEM((3, 8, 128), jnp.float32), in...  24.4 us
    pallas_call x1, Pallas kernels, on_device(): pl.pallas_call(unpack, out_shape=(jax.ShapeDtypeStruct((owned, PRED * PRE...  0.75 us

profile of v7, /device:TPU:1, one launch (start us, length us, event | category | flops | bytes accessed | tf_op | source)
XLA Modules:
  0.0 25.8 jit_solution(16743296741596626664)
XLA Ops:
  0.6 24.4 %normal_equations.1.sum_ref = f32[3,8,128]{2,1,0:T(8,128)S(1)} custom-call(bf16[2048,2048]{1,0:T(8,128)(2,1)} %dep_ref.1, bf16[10,2048]{1,0:T(8,128)(2,1)} %pred_hbm.1, bf16[63,2048]{1,0:T(8,128)(2,1)} %inv_hbm.1, s32[64,128]{1,0:T(8,128)} %bitcast.2, s32[16]{0:T(128)} %lines_hbm.1, bf16[16,256]{1,0:T(8,128)(2,1)} %constant.2.clone.sel_hbm), custom_call_target="tpu_custom_call" | custom-call | tf_op jit(solution)/shard_map/normal_equations/pallas_call | solution.py:512
  25.0 0.7 %unpack.1 = (f32[32,100]{1,0:T(8,128)}, f32[10,32]{1,0:T(8,128)}) custom-call(f32[3,8,128]{2,1,0:T(8,128)S(1)} %normal_equations.1.sum_ref), custom_call_target="tpu_custom_call" | custom-call | tf_op jit(solution)/shard_map/unpack/pallas_call | solution.py:569

commit v8 on v7

--- a/solution.py
+++ b/solution.py
@@ -387,8 +387,7 @@
             device_id_type=MESH,
         )
 
-    @pl.when(z != 4)
-    def _():
+    def pass_far_on():
         for n in range(len(FAR)):
             wait_for(far_recv.at[n], 7, far_recv_sem.at[n])
             chunk = far_own[n]
@@ -397,6 +396,10 @@
                 chunk = chunk + jnp.where(source == p, jnp.zeros_like(came), came)
             far_sum[n] = chunk
             far_copy(n).start()
+
+    @pl.when(z > 4)
+    def _():
+        pass_far_on()
 
     @pl.when(z > 0)
     def _():
@@ -423,6 +426,10 @@
             device_id=(z * 8 + peer, chan),
             device_id_type=MESH,
         ).start()
+
+    @pl.when(z < 4)
+    def _():
+        pass_far_on()
 
     mine = send2[p]
     @pl.when(z == 0)

time: 26.1 us -> 26.1 us (level)
  no operation moved by 1% of the time
where the time goes in v8:
time: 26.1 us; the launch traced here: 25.8 us
  Pallas kernels  25.1 us (96%)
  between operations  0.64 us (2%)
    pallas_call x1, Pallas kernels, on_device(): pl.pallas_call(kernel, out_shape=pltpu.VMEM((3, 8, 128), jnp.float32), in...  24.4 us
    pallas_call x1, Pallas kernels, on_device(): pl.pallas_call(unpack, out_shape=(jax.ShapeDtypeStruct((owned, PRED * PRE...  0.75 us

profile of v8, /device:TPU:1, one launch (start us, length us, event | category | flops | bytes accessed | tf_op | source)
XLA Modules:
  0.0 25.8 jit_solution(12535023486930873368)
XLA Ops:
  0.6 24.4 %normal_equations.1.sum_ref = f32[3,8,128]{2,1,0:T(8,128)S(1)} custom-call(bf16[2048,2048]{1,0:T(8,128)(2,1)} %dep_ref.1, bf16[10,2048]{1,0:T(8,128)(2,1)} %pred_hbm.1, bf16[63,2048]{1,0:T(8,128)(2,1)} %inv_hbm.1, s32[64,128]{1,0:T(8,128)} %bitcast.2, s32[16]{0:T(128)} %lines_hbm.1, bf16[16,256]{1,0:T(8,128)(2,1)} %constant.2.clone.sel_hbm), custom_call_target="tpu_custom_call" | custom-call | tf_op jit(solution)/shard_map/normal_equations/pallas_call | solution.py:519
  25.0 0.7 %unpack.1 = (f32[32,100]{1,0:T(8,128)}, f32[10,32]{1,0:T(8,128)}) custom-call(f32[3,8,128]{2,1,0:T(8,128)S(1)} %normal_equations.1.sum_ref), custom_call_target="tpu_custom_call" | custom-call | tf_op jit(solution)/shard_map/unpack/pallas_call | solution.py:576
